TPU v7x, 32 devices: a whole 2x2x4 slice. The times are simulated.
32 devices in a mesh: dp: 4 (over z), mp: 8 (over y, x, core).
Axes of the slice: x: 2, y: 2, z: 4, core: 2. Of those that a mesh axis runs over, the one named last changes fastest.
Arguments:
- patches: bfloat16 [4096, 1280], P(('dp', 'mp')), may hold values from -6 to 6
- window_ids: int32 [32, 128], P(('dp', 'mp')), may hold values from 0 to 7, never falling along the last dimension, each value on 1 to 64 neighbouring positions
- owner: int32 [1024, 1], P(('dp', 'mp')), may hold values from 0 to 3; in each aligned block of 32 rows (0 to 31, 32 to 63, ...) at most 16 rows name the same one
- slot_of_row: int32 [32, 64], P(('dp', 'mp')), may hold values from 0 to 63, each once within a row
- text_embeds: bfloat16 [2048, 8192], P(('dp', 'mp')), may hold values from -6 to 6
- vit_norm: float32 [1280], replicated, may hold values from 0.3 to 3
- vit_qkv_w: bfloat16 [1280, 1920], replicated, may hold values from -0.15625 to 0.15625
- vit_qkv_b: float32 [1920], replicated, may hold values from -12 to 12
- vit_out_w: bfloat16 [640, 1280], replicated, may hold values from -0.25 to 0.25
- merge_norm: float32 [1280], replicated, may hold values from 0.3 to 3
- merge_w1: bfloat16 [5120, 5120], P(None, 'mp'), may hold values from -0.078125 to 0.078125
- merge_b1: float32 [5120], P('mp'), may hold values from -3 to 3
- merge_w2: bfloat16 [5120, 8192], P('mp'), may hold values from -0.078125 to 0.078125
- merge_b2: float32 [8192], replicated, may hold values from -3 to 3
- llm_norm: float32 [8192], replicated, may hold values from 0.5 to 1.5
- q_w: bfloat16 [8192, 4096], P(None, 'mp'), may hold values from -0.0625 to 0.0625
- q_b: float32 [4096], P('mp'), may hold values from -12 to 12
- kv_w: bfloat16 [2, 8192, 512], P(None, None, 'mp'), may hold values from -0.0625 to 0.0625
- kv_b: float32 [2, 512], P(None, 'mp'), may hold values from -12 to 12
Outputs:
- attended: bfloat16 [2048, 4096], P('dp', 'mp')
Inputs may be any that keep to these rules, and one draw needn't show every extreme that they name: `window_ids`: within each block, window numbers never fall and each window has at most 64 patches. Among the 32 merged rows of one device, no owner is named by more than 16 rows, a bound that some block reaches. `slot_of_row`: each row is a permutation of the 64 slots.
All inputs are finite; a program needn't handle non-finite values.
Results may differ from a plain program's by a relative error of at most 0.04.
Values may be sent and summed in bfloat16 or wider, within the bound.
A program may use at most 128 MiB of HBM per device.

v0:
```python
import functools
import jax
import jax.numpy as jnp
from jax import lax
from jax.experimental import pallas as pl
from jax.experimental.pallas import tpu as pltpu
from jax.sharding import PartitionSpec as P

VHD = 80
HD = 128
QH = 32
KVH = 4

MESH = pl.DeviceIdType.MESH
LIMIT = 60 * 1024 * 1024


def corners():
    me = lax.axis_index("mp")
    core, first, second = me % 2, (me // 2) % 2, me // 4
    partner = 1 - 2 * core
    across = 2 - 4 * first
    up = 4 - 8 * second
    return me, partner, across, up


def greet(axis, others):
    barrier = pltpu.get_barrier_semaphore()
    for other in others:
        pl.semaphore_signal(barrier, inc=1, device_id={axis: other}, device_id_type=MESH)
    pl.semaphore_wait(barrier, len(others))


def gather_kernel(rows, in_ref, out_ref, local_sem, send_sem, recv_sem):
    me, partner, across, up = corners()
    greet("mp", (me + partner, me + across, me + up))
    half = rows // 2

    def piece(device, part):
        if part is None:
            return out_ref.at[pl.ds(pl.multiple_of(device * rows, rows), rows)]
        return out_ref.at[pl.ds(pl.multiple_of(device * rows + part * half, half), half)]

    def own(part):
        return in_ref if part is None else in_ref.at[pl.ds(part * half, half)]

    def copy(index, device, part, target, mine=False):
        return pltpu.make_async_remote_copy(
            src_ref=own(part) if mine else piece(device, part),
            dst_ref=piece(device, part),
            send_sem=send_sem.at[index],
            recv_sem=recv_sem.at[index],
            device_id={"mp": target},
            device_id_type=MESH,
        )

    x0 = copy(0, me, 0, me + across, True)
    y1 = copy(4, me, 1, me + up, True)
    x1 = copy(1, me, 1, me + across, True)
    y0 = copy(3, me, 0, me + up, True)
    mate = copy(6, me, None, me + partner, True)
    for item in (x0, y1, x1, y0, mate):
        item.start()
    keep = pltpu.make_async_copy(in_ref, piece(me, None), local_sem)
    keep.start()
    x0.wait_recv()
    far0 = copy(5, me + across, 0, me + up)
    far0.start()
    y1.wait_recv()
    far1 = copy(2, me + up, 1, me + across)
    far1.start()
    x1.wait_recv()
    mate_x = copy(7, me + across, None, me + partner)
    mate_x.start()
    y0.wait_recv()
    mate_y = copy(8, me + up, None, me + partner)
    mate_y.start()
    far0.wait_recv()
    mate_f0 = copy(9, me + across + up, 0, me + partner)
    mate_f0.start()
    far1.wait_recv()
    mate_f1 = copy(10, me + across + up, 1, me + partner)
    mate_f1.start()
    for item in (mate, mate_x, mate_y, mate_f0, mate_f1):
        item.wait_recv()
    for item in (x0, x1, y0, y1, far0, far1, mate, mate_x, mate_y, mate_f0, mate_f1):
        item.wait_send()
    keep.wait()


def gather_mp(block, collective_id):
    ranks = lax.axis_size("mp")
    if ranks != 8:
        return lax.all_gather(block, "mp", axis=0, tiled=True)
    rows, columns = block.shape
    return pl.pallas_call(
        functools.partial(gather_kernel, rows),
        out_shape=jax.ShapeDtypeStruct((ranks * rows, columns), block.dtype),
        in_specs=[pl.BlockSpec(memory_space=pltpu.VMEM)],
        out_specs=pl.BlockSpec(memory_space=pl.ANY),
        scratch_shapes=[
            pltpu.SemaphoreType.DMA,
            pltpu.SemaphoreType.DMA((11,)),
            pltpu.SemaphoreType.DMA((11,)),
        ],
        compiler_params=pltpu.CompilerParams(collective_id=collective_id, has_side_effects=True),
        cost_estimate=pl.CostEstimate(flops=0, bytes_accessed=ranks * block.size * 2, transcendentals=0),
    )(block)


def scatter_kernel(in_ref, out_ref, mate_ref, sum_ref, in_x, in_y, via_ref, last_ref, send_sem, recv_sem):
    me, partner, across, up = corners()
    greet("mp", (me + partner, me + across, me + up))
    columns = in_ref.shape[2]
    half = columns // 2
    step = min(half, 1024)
    devices = (me + across + up, me + across, me + up, me)

    def copy(index, src, dst, target):
        return pltpu.make_async_remote_copy(
            src_ref=src, dst_ref=dst, send_sem=send_sem.at[index], recv_sem=recv_sem.at[index],
            device_id={"mp": target}, device_id_type=MESH,
        )

    def tiles(body):
        def run(i, carry):
            body(pl.multiple_of(i * step, step))
            return carry
        lax.fori_loop(0, half // step, run, 0)

    mates = []
    for slot in range(4):
        item = copy(slot, in_ref.at[devices[slot] + partner], mate_ref.at[slot], me + partner)
        item.start()
        mates.append(item)

    def add_mate(slot):
        mates[slot].wait_recv()
        for part in range(2):
            def body(at):
                cut = pl.ds(part * half + at, step)
                sum_ref[slot, :, cut] = (
                    in_ref[devices[slot], :, cut].astype(jnp.float32) + mate_ref[slot, :, cut].astype(jnp.float32)
                ).astype(jnp.bfloat16)
            tiles(body)

    low, high = pl.ds(0, half), pl.ds(half, half)
    add_mate(0)
    far_x = copy(4, sum_ref.at[0, :, low], in_x.at[0], me + across)
    far_x.start()
    far_y = copy(5, sum_ref.at[0, :, high], in_y.at[0], me + up)
    far_y.start()
    add_mate(1)
    near_x = copy(6, sum_ref.at[1, :, low], in_x.at[1], me + across)
    near_x.start()
    add_mate(2)
    near_y = copy(7, sum_ref.at[2, :, high], in_y.at[1], me + up)
    near_y.start()
    add_mate(3)
    far_x.wait_recv()

    def via_low(at):
        cut = pl.ds(at, step)
        via_ref[0, :, cut] = (
            sum_ref[2, :, cut].astype(jnp.float32) + in_x[0, :, cut].astype(jnp.float32)
        ).astype(jnp.bfloat16)
    tiles(via_low)
    last_y = copy(8, via_ref.at[0], last_ref.at[0], me + up)
    last_y.start()
    far_y.wait_recv()

    def via_high(at):
        cut = pl.ds(at, step)
        via_ref[1, :, cut] = (
            sum_ref[1, :, pl.ds(half + at, step)].astype(jnp.float32) + in_y[0, :, cut].astype(jnp.float32)
        ).astype(jnp.bfloat16)
    tiles(via_high)
    last_x = copy(9, via_ref.at[1], last_ref.at[1], me + across)
    last_x.start()
    near_x.wait_recv()
    last_y.wait_recv()

    def own_low(at):
        cut = pl.ds(at, step)
        out_ref[:, cut] = (
            sum_ref[3, :, cut].astype(jnp.float32)
            + in_x[1, :, cut].astype(jnp.float32) + last_ref[0, :, cut].astype(jnp.float32)
        )
    tiles(own_low)
    near_y.wait_recv()
    last_x.wait_recv()

    def own_high(at):
        cut, wide = pl.ds(at, step), pl.ds(half + at, step)
        out_ref[:, wide] = (
            sum_ref[3, :, wide].astype(jnp.float32)
            + in_y[1, :, cut].astype(jnp.float32) + last_ref[1, :, cut].astype(jnp.float32)
        )
    tiles(own_high)
    for item in mates + [far_x, far_y, near_x, near_y, last_x, last_y]:
        item.wait_send()


def scatter_mp(partial, collective_id):
    ranks = lax.axis_size("mp")
    if ranks != 8:
        return lax.psum_scatter(partial, "mp", scatter_dimension=0, tiled=True).astype(jnp.float32)
    rows, columns = partial.shape[0] // ranks, partial.shape[1]
    half = columns // 2
    return pl.pallas_call(
        scatter_kernel,
        out_shape=jax.ShapeDtypeStruct((rows, columns), jnp.float32),
        in_specs=[pl.BlockSpec(memory_space=pltpu.VMEM)],
        out_specs=pl.BlockSpec(memory_space=pltpu.VMEM),
        scratch_shapes=[
            pltpu.VMEM((4, rows, columns), jnp.bfloat16),
            pltpu.VMEM((4, rows, columns), jnp.bfloat16),
            pltpu.VMEM((2, rows, half), jnp.bfloat16),
            pltpu.VMEM((2, rows, half), jnp.bfloat16),
            pltpu.VMEM((2, rows, half), jnp.bfloat16),
            pltpu.VMEM((2, rows, half), jnp.bfloat16),
            pltpu.SemaphoreType.DMA((10,)),
            pltpu.SemaphoreType.DMA((10,)),
        ],
        compiler_params=pltpu.CompilerParams(collective_id=collective_id, has_side_effects=True),
        cost_estimate=pl.CostEstimate(flops=0, bytes_accessed=partial.size * 4, transcendentals=0),
    )(partial.reshape(ranks, rows, columns))


def exchange_kernel(axis, ranks, pick, count, *refs):
    ins, outs = refs[:count], refs[count:2 * count]
    local_sem, send_sem, recv_sem = refs[2 * count:]
    me = lax.axis_index(axis)
    targets = [lax.rem(me + step, ranks) for step in range(1, ranks)]
    greet(axis, targets)
    copies = []
    for index in range(count):
        for place, target in enumerate(targets):
            item = pltpu.make_async_remote_copy(
                src_ref=ins[index].at[pick(target)], dst_ref=outs[index].at[me],
                send_sem=send_sem.at[index, place], recv_sem=recv_sem.at[index, place],
                device_id={axis: target}, device_id_type=MESH,
            )
            item.start()
            copies.append(item)
        item = pltpu.make_async_copy(ins[index].at[pick(me)], outs[index].at[me], local_sem.at[index])
        item.start()
        copies.append(item)
    for item in copies:
        item.wait()


def exchange(arrays, axis, pick, collective_id):
    ranks = lax.axis_size(axis)
    return pl.pallas_call(
        functools.partial(exchange_kernel, axis, ranks, pick, len(arrays)),
        out_shape=[jax.ShapeDtypeStruct((ranks,) + a.shape[1:], a.dtype) for a in arrays],
        in_specs=[pl.BlockSpec(memory_space=pltpu.VMEM)] * len(arrays),
        out_specs=[pl.BlockSpec(memory_space=pltpu.VMEM)] * len(arrays),
        scratch_shapes=[
            pltpu.SemaphoreType.DMA((len(arrays),)),
            pltpu.SemaphoreType.DMA((len(arrays), ranks - 1)),
            pltpu.SemaphoreType.DMA((len(arrays), ranks - 1)),
        ],
        compiler_params=pltpu.CompilerParams(collective_id=collective_id, has_side_effects=True),
        cost_estimate=pl.CostEstimate(flops=0, bytes_accessed=4 * sum(a.size for a in arrays), transcendentals=0),
    )(*arrays)


CHUNKS = 4


def handover_kernel(
    groups, ranks, emb_ref, selector_ref, marks_ref, picker_ref, text_ref, gain_ref, q_ref, kv_ref,
    out_ref, square_ref,
    send_ref, arrived_ref, arrived_marks, rows_ref, q_here, kv_here, own_square,
    load_sem, z_send, z_recv, send_sem, recv_sem, s_send, s_recv,
):
    me, partner, across, up = corners()
    group = lax.axis_index("dp")
    peers = [lax.rem(group + step, groups) for step in range(1, groups)]
    others = [lax.rem(me + step, ranks) for step in range(1, ranks)]
    loads = [pltpu.make_async_copy(q_ref, q_here, load_sem.at[0]), pltpu.make_async_copy(kv_ref, kv_here, load_sem.at[1])]
    for item in loads:
        item.start()
    barrier = pltpu.get_barrier_semaphore()
    for peer in peers:
        pl.semaphore_signal(barrier, inc=1, device_id={"dp": peer}, device_id_type=MESH)
    for other in others:
        pl.semaphore_signal(barrier, inc=1, device_id={"mp": other}, device_id_type=MESH)
    pl.semaphore_wait(barrier, groups + ranks - 2)

    slots, width = text_ref.shape
    room = slots // groups
    wide = width // CHUNKS
    half = slots // 2

    def block_of(index):
        return pl.ds(pl.multiple_of(index * room, room), room)

    own_block = block_of(group)
    pending = []

    def z_copy(index, place, src, dst):
        item = pltpu.make_async_remote_copy(
            src_ref=src, dst_ref=dst, send_sem=z_send.at[index, place], recv_sem=z_recv.at[index, place],
            device_id={"dp": peers[place]}, device_id_type=MESH,
        )
        item.start()
        pending.append(item)
        return item

    mark_copies = [
        z_copy(CHUNKS, place, marks_ref.at[block_of(peers[place])], arrived_marks.at[own_block])
        for place in range(groups - 1)
    ]
    arrived_marks[own_block, :] = marks_ref[own_block, :]
    z_copies = []
    for chunk in range(CHUNKS):
        cut = pl.ds(chunk * wide, wide)
        send_ref[:, cut] = jnp.dot(
            selector_ref[...], emb_ref[:, cut], preferred_element_type=jnp.float32
        ).astype(jnp.bfloat16)
        z_copies.append([
            z_copy(chunk, place, send_ref.at[block_of(peers[place]), cut], arrived_ref.at[own_block, cut])
            for place in range(groups - 1)
        ])
        arrived_ref[own_block, cut] = send_ref[own_block, cut]

    def piece(device, part, cut):
        if part is None:
            return rows_ref.at[pl.ds(pl.multiple_of(device * slots, slots), slots), cut]
        return rows_ref.at[pl.ds(pl.multiple_of(device * slots + part * half, half), half), cut]

    def copy(chunk, index, device, part, target):
        ref = piece(device, part, pl.ds(chunk * wide, wide))
        item = pltpu.make_async_remote_copy(
            src_ref=ref, dst_ref=ref, send_sem=send_sem.at[chunk, index], recv_sem=recv_sem.at[chunk, index],
            device_id={"mp": target}, device_id_type=MESH,
        )
        item.start()
        pending.append(item)
        return item

    for item in mark_copies:
        item.wait_recv()
    image_here = jnp.dot(picker_ref[...], arrived_marks[...], preferred_element_type=jnp.float32)[:, :1] > 0.5
    own_square[...] = jnp.zeros_like(own_square)
    firsts, mates = [], []

    def choose(chunk):
        cut = pl.ds(chunk * wide, wide)
        for item in z_copies[chunk]:
            item.wait_recv()
        picked = jnp.dot(picker_ref[...], arrived_ref[:, cut], preferred_element_type=jnp.float32)
        sequence = jnp.where(image_here, picked, text_ref[:, cut].astype(jnp.float32))
        squares = sequence * sequence
        total = squares[:, :128]
        for at in range(128, wide, 128):
            total = total + squares[:, at:at + 128]
        own_square[pl.ds(0, slots), :] += total
        rows_ref[pl.ds(pl.multiple_of(me * slots, slots), slots), cut] = (
            sequence * gain_ref[:, cut]
        ).astype(jnp.bfloat16)
        x0 = copy(chunk, 0, me, 0, me + across)
        y1 = copy(chunk, 4, me, 1, me + up)
        x1 = copy(chunk, 1, me, 1, me + across)
        y0 = copy(chunk, 3, me, 0, me + up)
        mate = copy(chunk, 6, me, None, me + partner)
        firsts.append((x0, y1, x1, y0))
        mates.append([mate])

    def forward(chunk):
        x0, y1, x1, y0 = firsts[chunk]
        x0.wait_recv()
        far0 = copy(chunk, 5, me + across, 0, me + up)
        y1.wait_recv()
        far1 = copy(chunk, 2, me + up, 1, me + across)
        x1.wait_recv()
        mates[chunk].append(copy(chunk, 7, me + across, None, me + partner))
        y0.wait_recv()
        mates[chunk].append(copy(chunk, 8, me + up, None, me + partner))
        firsts[chunk] = (far0, far1)

    def corner(chunk):
        far0, far1 = firsts[chunk]
        far0.wait_recv()
        mates[chunk].append(copy(chunk, 9, me + across + up, 0, me + partner))
        far1.wait_recv()
        mates[chunk].append(copy(chunk, 10, me + across + up, 1, me + partner))

    queries = q_here.shape[1]
    height = 256

    def project(chunk):
        cut = pl.ds(chunk * wide, wide)
        for item in mates[chunk]:
            item.wait_recv()
        if chunk == 0:
            for item in loads:
                item.wait()

        def run(i, carry):
            some = pl.ds(pl.multiple_of(i * height, height), height)
            left = jnp.dot(rows_ref[some, cut], q_here[cut, :], preferred_element_type=jnp.float32)
            right = jnp.dot(rows_ref[some, cut], kv_here[cut, :], preferred_element_type=jnp.float32)
            if chunk:
                left = left + out_ref[some, pl.ds(0, queries)]
                right = right + out_ref[some, pl.ds(queries, kv_here.shape[1])]
            out_ref[some, pl.ds(0, queries)] = left
            out_ref[some, pl.ds(queries, kv_here.shape[1])] = right
            return carry
        lax.fori_loop(0, ranks * slots // height, run, 0)

    for chunk in range(CHUNKS):
        choose(chunk)
        if chunk > 0:
            forward(chunk - 1)
        if chunk > 1:
            corner(chunk - 2)
            project(chunk - 2)
    square_ref[me] = jnp.broadcast_to(jnp.sum(own_square[...].T, axis=0, keepdims=True), square_ref.shape[1:])
    forward(CHUNKS - 1)
    square_copies = []
    for place, other in enumerate(others):
        item = pltpu.make_async_remote_copy(
            src_ref=square_ref.at[me], dst_ref=square_ref.at[me], send_sem=s_send.at[place], recv_sem=s_recv.at[place],
            device_id={"mp": other}, device_id_type=MESH,
        )
        item.start()
        square_copies.append(item)
    corner(CHUNKS - 2)
    project(CHUNKS - 2)
    corner(CHUNKS - 1)
    project(CHUNKS - 1)
    for item in square_copies:
        item.wait()
    for item in pending:
        item.wait_send()


def handover(embedded, selector, picker, text, gain, q_w, kv_both, collective_id):
    groups, ranks = lax.axis_size("dp"), lax.axis_size("mp")
    slots, width = text.shape
    marks = jnp.broadcast_to(jnp.sum(selector, axis=1, keepdims=True), (slots, 128)).astype(jnp.bfloat16)
    columns = q_w.shape[1] + kv_both.shape[1]
    vmem = pl.BlockSpec(memory_space=pltpu.VMEM)
    hbm = pl.BlockSpec(memory_space=pl.ANY)
    return pl.pallas_call(
        functools.partial(handover_kernel, groups, ranks),
        out_shape=[
            jax.ShapeDtypeStruct((ranks * slots, columns), jnp.float32),
            jax.ShapeDtypeStruct((ranks, 8, 128), jnp.float32),
        ],
        in_specs=[vmem] * 6 + [hbm] * 2,
        out_specs=[vmem] * 2,
        scratch_shapes=[
            pltpu.VMEM((slots, width), jnp.bfloat16),
            pltpu.VMEM((slots, width), jnp.bfloat16),
            pltpu.VMEM((slots, 128), jnp.bfloat16),
            pltpu.VMEM((ranks * slots, width), jnp.bfloat16),
            pltpu.VMEM(q_w.shape, q_w.dtype),
            pltpu.VMEM(kv_both.shape, kv_both.dtype),
            pltpu.VMEM((128, 128), jnp.float32),
            pltpu.SemaphoreType.DMA((2,)),
            pltpu.SemaphoreType.DMA((CHUNKS + 1, groups - 1)),
            pltpu.SemaphoreType.DMA((CHUNKS + 1, groups - 1)),
            pltpu.SemaphoreType.DMA((CHUNKS, 11)),
            pltpu.SemaphoreType.DMA((CHUNKS, 11)),
            pltpu.SemaphoreType.DMA((ranks - 1,)),
            pltpu.SemaphoreType.DMA((ranks - 1,)),
        ],
        compiler_params=pltpu.CompilerParams(collective_id=collective_id, has_side_effects=True, vmem_limit_bytes=LIMIT),
        cost_estimate=pl.CostEstimate(flops=2 * ranks * slots * width * columns, bytes_accessed=12 * ranks * slots * width, transcendentals=0),
    )(embedded, selector.astype(jnp.bfloat16), marks, picker.astype(jnp.bfloat16), text, gain.reshape(1, -1), q_w, kv_both)


epsilon = 1e-06


def rms_norm(inputs, gain):
    inputs = inputs.astype(jnp.float32)
    return inputs * lax.rsqrt(jnp.mean(inputs * inputs, axis=-1, keepdims=True) + epsilon) * gain


def vision_block(patches, window_ids, vit_norm, vit_qkv_w, vit_qkv_b, vit_out_w, merge_norm):
    normed = rms_norm(patches, vit_norm).astype(jnp.bfloat16)
    projected = (jnp.dot(normed, vit_qkv_w, preferred_element_type=jnp.float32) + vit_qkv_b).astype(
        jnp.bfloat16
    )
    blocks = window_ids.shape[0]
    width = window_ids.shape[1]
    inner_width = vit_out_w.shape[0]
    heads = inner_width // VHD
    shaped = projected.reshape(blocks, width, 3, heads, VHD)
    scores = jnp.einsum(
        "bqhd,bkhd->bhqk", shaped[:, :, 0], shaped[:, :, 1], preferred_element_type=jnp.float32
    ) * VHD ** (-0.5)
    in_window = window_ids[:, None, :, None] == window_ids[:, None, None, :]
    scores = jnp.where(in_window, scores, -1e30)
    peak = jnp.max(scores, axis=-1, keepdims=True)
    weights = jnp.exp(scores - peak)
    weights = (weights / jnp.sum(weights, axis=-1, keepdims=True)).astype(jnp.bfloat16)
    mixture = jnp.einsum(
        "bhqk,bkhd->bqhd", weights, shaped[:, :, 2], preferred_element_type=jnp.float32
    )
    mixture = mixture.astype(jnp.bfloat16).reshape(blocks * width, inner_width)
    residual = (
        patches.astype(jnp.float32)
        + jnp.dot(mixture, vit_out_w, preferred_element_type=jnp.float32)
    ).astype(jnp.bfloat16)
    merged = rms_norm(residual, merge_norm).astype(jnp.bfloat16)
    return merged.reshape(blocks * width // 4, 4 * patches.shape[1])


def shards(
    patches,
    window_ids,
    owner,
    slot_of_row,
    text_embeds,
    vit_norm,
    vit_qkv_w,
    vit_qkv_b,
    vit_out_w,
    merge_norm,
    merge_w1,
    merge_b1,
    merge_w2,
    merge_b2,
    llm_norm,
    q_w,
    q_b,
    kv_w,
    kv_b,
):
    merged = vision_block(
        patches, window_ids, vit_norm, vit_qkv_w, vit_qkv_b, vit_out_w, merge_norm
    )
    rows_all = gather_mp(merged, 0)
    hidden = jax.nn.gelu(
        jnp.dot(rows_all, merge_w1, preferred_element_type=jnp.float32) + merge_b1,
        approximate=False,
    ).astype(jnp.bfloat16)
    own_rows = scatter_mp(
        jnp.dot(hidden, merge_w2, preferred_element_type=jnp.float32).astype(jnp.bfloat16), 1
    )
    embedded = (own_rows + merge_b2).astype(jnp.bfloat16)
    seq_rows = text_embeds.shape[0]
    groups = lax.axis_size("dp")
    capacity = seq_rows // groups
    target_group = owner[:, 0]
    onehot = (target_group[:, None] == jnp.arange(groups, dtype=jnp.int32)[None, :]).astype(
        jnp.int32
    )
    rank_in = jnp.sum((jnp.cumsum(onehot, axis=0) - onehot) * onehot, axis=1)
    send_slot = target_group * capacity + rank_in
    selector = send_slot[None, :] == jnp.arange(seq_rows, dtype=jnp.int32)[:, None]
    query_cols = q_w.shape[1]
    kv_cols = kv_w.shape[2]
    if lax.axis_size("mp") == 8:
        picker = slot_of_row[0][:, None] == jnp.arange(seq_rows, dtype=jnp.int32)[None, :]
        kv_both = jnp.concatenate([kv_w[0], kv_w[1]], axis=1)
        projected, squares = handover(embedded, selector, picker, text_embeds, llm_norm, q_w, kv_both, 2)
        squares = squares[:, 0, :seq_rows].reshape(-1, 1)
        projected = projected * lax.rsqrt(squares / text_embeds.shape[1] + epsilon)
    else:
        buffer = jnp.dot(
            selector.astype(jnp.bfloat16), embedded, preferred_element_type=jnp.float32
        ).astype(jnp.bfloat16)
        buffer = buffer.reshape(groups, capacity, embedded.shape[1])
        counts = jnp.broadcast_to(jnp.sum(onehot, axis=0)[:, None, None], (groups, 8, 128))
        arrived, arrived_counts = exchange((buffer, counts), "dp", lambda target: target, 2)
        arrived = arrived.reshape(seq_rows, embedded.shape[1])
        chosen = slot_of_row[0]
        places = jnp.arange(seq_rows, dtype=jnp.int32)
        filled = places % capacity < jnp.repeat(arrived_counts[:, 0, 0], capacity)
        chooser = (chosen[:, None] == places[None, :]) & filled[None, :]
        picked = jnp.dot(chooser.astype(jnp.bfloat16), arrived, preferred_element_type=jnp.float32)
        image_here = jnp.any(chooser, axis=1)[:, None]
        sequence = jnp.where(image_here, picked, text_embeds.astype(jnp.float32))
        llm_normed = rms_norm(sequence, llm_norm).astype(jnp.bfloat16)
        shard_rows = gather_mp(llm_normed, 3)
        projected = jnp.concatenate(
            [
                jnp.dot(shard_rows, q_w, preferred_element_type=jnp.float32),
                jnp.dot(shard_rows, kv_w[0], preferred_element_type=jnp.float32),
                jnp.dot(shard_rows, kv_w[1], preferred_element_type=jnp.float32),
            ],
            axis=1,
        )
    length = projected.shape[0]
    queries = (projected[:, :query_cols] + q_b).astype(jnp.bfloat16)
    key_rows = (projected[:, query_cols : query_cols + kv_cols] + kv_b[0]).astype(jnp.bfloat16)
    value_rows = (projected[:, query_cols + kv_cols :] + kv_b[1]).astype(jnp.bfloat16)
    heads_here = query_cols // HD
    group_size = QH // KVH
    dims_here = kv_cols // KVH

    def head_major(columns):
        return columns.T.reshape(dims_here, KVH, length).swapaxes(0, 1)

    stacked = jnp.stack([head_major(key_rows), head_major(value_rows)], axis=1)
    (own_head,) = exchange((stacked,), "mp", lambda target: target * heads_here // group_size, 4)
    key_cols = own_head[:, 0].reshape(HD, length)
    value_cols = own_head[:, 1].reshape(HD, length)
    query_heads = queries.reshape(length, heads_here, HD)
    scores = jnp.einsum(
        "qhd,dk->hqk", query_heads, key_cols, preferred_element_type=jnp.float32
    ) * HD ** (-0.5)
    allowed = jnp.arange(length)[:, None] >= jnp.arange(length)[None, :]
    scores = jnp.where(allowed[None], scores, -1e30)
    peak = jnp.max(scores, axis=-1, keepdims=True)
    weights = jnp.exp(scores - peak)
    weights = (weights / jnp.sum(weights, axis=-1, keepdims=True)).astype(jnp.bfloat16)
    mixture = jnp.einsum("hqk,dk->qhd", weights, value_cols, preferred_element_type=jnp.float32)
    return mixture.astype(jnp.bfloat16).reshape(length, query_cols)


def solution(mesh):
    return jax.shard_map(
        shards,
        mesh=mesh,
        in_specs=(
            P(("dp", "mp"), None),
            P(("dp", "mp"), None),
            P(("dp", "mp"), None),
            P(("dp", "mp"), None),
            P(("dp", "mp"), None),
            P(),
            P(),
            P(),
            P(),
            P(),
            P(None, "mp"),
            P("mp"),
            P("mp", None),
            P(),
            P(),
            P(None, "mp"),
            P("mp"),
            P(None, None, "mp"),
            P(None, "mp"),
        ),
        out_specs=P("dp", "mp"),
        check_vma=False,
    )
```

profile of v0, /device:TPU:0, one launch (start us, length us, event | category | flops | bytes accessed | tf_op | source)
XLA Modules:
  0.0 154.1 jit_solution(3109318997588512251)
XLA Ops:
  0.0 0.9 broadcast_compare_fusion
  0.9 1.1 fusion.15
  2.0 3.5 %fusion.5 = bf16[128,1920]{1,0:T(8,128)(2,1)S(1)} fusion(bf16[1280,1920]{1,0:T(8,128)(2,1)} %param.25, f32[1920]{0:T(1024)} %param.26, bf16[128,1280]{1,0:T(8,128)(2,1)} %param.19, f32[1280]{0:T(1024)} %param.24, f32[128]{0:T(128)S(1)} %add_rsqrt_fusion.1), kind=kOutput, calls=%fused_computation.11 | convolution fusion | flops 630292480 | bytes 5747712 | tf_op jit(solution)/shard_map/dot_general | solution.py:488
  7.5 0.9 reshape.165.in_ref
  8.4 18.3 %shard_map.181 = bf16[256,5120]{1,0:T(8,128)(2,1)} custom-call(bf16[32,5120]{1,0:T(8,128)(2,1)} %reshape.165.in_ref), custom_call_target="tpu_custom_call" | custom-call | bytes 2621440 | tf_op jit(solution)/shard_map/pallas_call | solution.py:96
  26.7 17.2 %convolution_convert_fusion = bf16[256,8192]{1,0:T(8,128)(2,1)} fusion(bf16[640,8192]{1,0:T(8,128)(2,1)} %param.31, bf16[256,5120]{1,0:T(8,128)(2,1)} %shard_map.181, bf16[5120,640]{1,0:T(8,128)(2,1)} %param.29, f32[640]{0:T(1024)S(1)} %copy-done.10), kind=kOutput, calls=%fused_computation.2 | convolution fusion | flops 4374986752 | bytes 23857664 | tf_op jit(solution)/shard_map/dot_general | solution.py:546
  43.9 25.5 %shard_map.182 = f32[32,8192]{1,0:T(8,128)} custom-call(bf16[8,32,8192]{2,1,0:T(8,128)(2,1)} %bitcast.85), custom_call_target="tpu_custom_call" | custom-call | bytes 8388608 | tf_op jit(solution)/shard_map/pallas_call | solution.py:210
  69.5 2.1 %add_convert_fusion.emb_ref = bf16[32,8192]{1,0:T(8,128)(2,1)} fusion(f32[32,8192]{1,0:T(8,128)} %shard_map.182, f32[8192]{0:T(1024)S(1)} %copy-done.4), kind=kLoop, calls=%fused_computation.27 | loop fusion | flops 524288 | bytes 1605632 | tf_op jit(solution)/shard_map/convert_element_type | solution.py:548
  71.9 0.6 fusion.70.selector_ref
  72.6 0.7 broadcast_in_dim.24.marks_ref
  73.3 0.7 fusion.71.picker_ref
  74.0 1.2 fusion.108
  75.1 2.0 %copy.47 = bf16[1,8192,64]{2,1,0:T(8,128)(2,1)S(1)} copy(bf16[1,8192,64]{1,2,0:T(8,128)(2,1)} %get-tuple-element.10) | data formatting | bytes 2097152
  77.2 1.8 %copy.46 = bf16[1,8192,64]{2,1,0:T(8,128)(2,1)} copy(bf16[1,8192,64]{1,2,0:T(8,128)(2,1)S(1)} %get-tuple-element.9) | data formatting | bytes 2097152
  78.9 4.1 %pad_maximum_fusion.kv_ref = bf16[8192,128]{1,0:T(8,128)(2,1)} fusion(bf16[8192,64]{1,0:T(8,128)(2,1)S(1)} %bitcast.83, bf16[8192,64]{1,0:T(8,128)(2,1)} %bitcast.84), kind=kLoop, calls=%fused_computation.12 | loop fusion | flops 4194304 | bytes 4194304 | tf_op jit(solution)/shard_map/concatenate | solution.py:563
  83.0 54.5 %shard_map.183 = (f32[512,640]{1,0:T(8,128)}, f32[8,8,128]{2,1,0:T(8,128)}) custom-call(bf16[32,8192]{1,0:T(8,128)(2,1)} %add_convert_fusion.emb_ref, bf16[64,32]{1,0:T(8,128)(2,1)} %fusion.70.selector_ref, bf16[64,128]{1,0:T(8,128)(2,1)} %broadcast_in_dim.24.marks_ref, bf16[64,64]{1,0:T(8,128)(2,1)} %fusion.71.picker_ref, bf16[64,8192]{1,0:T(8,128)(2,1)} %text_ref.1, ...), custom_call_target="tpu_custom_call" | custom-call | flops 5368709120 | bytes 50331648 | tf_op jit(solution)/shard_map/pallas_call | solution.py:449
  137.5 0.8 rsqrt_reduce_fusion
  138.4 1.5 broadcast_multiply_fusion
  140.3 0.7 pad_maximum_fusion.1.refs_0_
  141.0 7.7 %shard_map.184 = bf16[8,2,16,512]{3,2,1,0:T(8,128)(2,1)} custom-call(bf16[4,2,16,512]{3,2,1,0:T(8,128)(2,1)} %pad_maximum_fusion.1.refs_0_), custom_call_target="tpu_custom_call" | custom-call | bytes 262144 | tf_op jit(solution)/shard_map/pallas_call | solution.py:255
  148.7 1.0 fusion.109
  149.7 0.7 fusion.29
  150.5 2.1 %fusion.111 = (f32[4,512]{1,0:T(4,128)S(1)}, f32[4,512,512]{1,2,0:T(8,128)S(1)}) fusion(f32[512,512,4]{1,0,2:T(8,128)S(1)} %fusion.29, pred[512,512]{0,1:T(8,128)(4,1)S(1)} %iota_compare_fusion), kind=kOutput, calls=%fused_computation.158 | output fusion | flops 6291967 | bytes 8658944 | tf_op jit(solution)/shard_map/sub | solution.py:614
  153.1 1.0 copy.41
  (46 shorter events, 3.4 us)
Async XLA Ops:
  0.0 6.8 %copy-start = (bf16[640,1280]{1,0:T(8,128)(2,1)S(1)}, bf16[640,1280]{1,0:T(8,128)(2,1)}, u32[]{:S(2)}) copy-start(bf16[640,1280]{1,0:T(8,128)(2,1)} %param.27) | copy-start | bytes 4915204
  5.5 1.3 copy-start.2
  5.5 1.8 %copy-start.5 = (f32[1280]{0:T(1024)S(1)}, f32[1280]{0:T(1024)}, u32[]{:S(2)}) copy-start(f32[1280]{0:T(1024)} %param.28) | copy-start | bytes 15364
  6.8 20.0 %copy-start.10 = (f32[640]{0:T(1024)S(1)}, f32[640]{0:T(1024)}, u32[]{:S(2)}) copy-start(f32[640]{0:T(1024)} %param.30) | copy-start | bytes 7684
  43.9 25.5 %copy-start.4 = (f32[8192]{0:T(1024)S(1)}, f32[8192]{0:T(1024)}, u32[]{:S(2)}) copy-start(f32[8192]{0:T(1024)} %param.32) | copy-start | bytes 98308
  43.9 27.6 %copy-start.7 = (s32[32,1]{0,1:T(1,128)S(1)}, s32[32,1]{0,1:T(1,128)}, u32[]{:S(2)}) copy-start(s32[32,1]{0,1:T(1,128)} %param.21) | copy-start | bytes 388
  43.9 29.4 %copy-start.9 = (s32[1,64]{1,0:T(1,128)S(1)}, s32[1,64]{1,0:T(1,128)}, u32[]{:S(2)}) copy-start(s32[1,64]{1,0:T(1,128)} %param.22) | copy-start | bytes 772
  43.9 30.1 %copy-start.3 = (bf16[2,8192,64]{1,2,0:T(8,128)(2,1)S(1)}, bf16[2,8192,64]{1,2,0:T(8,128)(2,1)}, u32[]{:S(2)}) copy-start(bf16[2,8192,64]{1,2,0:T(8,128)(2,1)} %param.36) | copy-start | bytes 6291460
  83.0 56.8 %copy-start.8 = (f32[2,64]{1,0:T(2,128)S(1)}, f32[2,64]{1,0:T(2,128)}, u32[]{:S(2)}) copy-start(f32[2,64]{1,0:T(2,128)} %param.37) | copy-start | bytes 1540
  137.5 12.2 %copy-start.6 = (f32[512]{0:T(512)S(1)}, f32[512]{0:T(512)}, u32[]{:S(2)}) copy-start(f32[512]{0:T(512)} %param.35) | copy-start | bytes 6148
  152.7 1.5 copy-start.1
where the time goes:
time: 156 us; the launch traced here: 154 us
  Pallas kernels  106 us (68%)
  matrix products  23.3 us (15%)
  other arithmetic  15.3 us (10%)
  local copies, waits for them, and re-layouts  9.25 us (6%)
    pallas_call x1, Pallas kernels, handover(): pl.pallas_call(functools.partial(handover_kernel, groups, ranks), out_sha...  54.5 us
    pallas_call x1, Pallas kernels, scatter_mp(): pl.pallas_call(scatter_kernel, out_shape=jax.ShapeDtypeStruct((rows, colu...  25.5 us
    pallas_call x1, Pallas kernels, gather_mp(): pl.pallas_call(functools.partial(gather_kernel, rows), out_shape=jax.Shap...  18.3 us
    dot_general x1, matrix products, shards(): jnp.dot(hidden, merge_w2, preferred_element_type=jnp.float32)  17.2 us
    pallas_call x1, Pallas kernels, exchange(): pl.pallas_call(functools.partial(exchange_kernel, axis, ranks, pick, len(...  7.7 us
    concatenate x1, other arithmetic, shards(): kv_both = jnp.concatenate([kv_w[0], kv_w[1]], axis=1)  4.09 us
    unnamed x24, local copies, waits for them, and re-layouts  3.85 us
    dot_general x1, matrix products, vision_block(): jnp.dot(normed, vit_qkv_w, preferred_element_type=jnp.float32) + vit_qkv_b  3.47 us

commit v1 on v0

--- a/solution.py
+++ b/solution.py
@@ -477,6 +477,446 @@
 
 epsilon = 1e-06
 
+STEPS = 8
+WIDE = 256
+TOP = 63 * 1024 * 1024
+
+
+def tiles_of(width):
+    return [(at, min(WIDE, width - at)) for at in range(0, width, WIDE)]
+
+
+def fused_kernel(
+    groups, ranks, steps, parts,
+    merged_ref, owner_ref, slots_ref, b1_ref, b2_ref, gain_ref, qb_ref, kvb_ref,
+    w1_hbm, w2_hbm, q_hbm, kv_hbm, text_hbm,
+    out_ref,
+    w1_ref, w2_ref, q_ref, kv_raw, kv_ref, text_ref,
+    all_ref, hidden_acc, hidden_ref, partial_ref, mate_ref, in_x, in_y, last_ref,
+    send_ref, arrived_ref, marks_ref, arrived_marks, rows_ref, acc_ref, own_square, square_ref,
+    turned_ref, heads_ref, query_ref,
+    load_sem, g_send, g_recv, r_send, r_recv, z_send, z_recv, a_send, a_recv, s_send, s_recv, k_send, k_recv,
+):
+    me, partner, across, up = corners()
+    group = lax.axis_index("dp")
+    peers = [lax.rem(group + step, groups) for step in range(1, groups)]
+    others = [lax.rem(me + step, ranks) for step in range(1, ranks)]
+    loads = [
+        pltpu.make_async_copy(src, dst, load_sem.at[at])
+        for at, (src, dst) in enumerate((
+            (w1_hbm, w1_ref), (kv_hbm, kv_raw), (w2_hbm, w2_ref), (text_hbm, text_ref), (q_hbm, q_ref),
+        ))
+    ]
+    for item in loads:
+        item.start()
+    barrier = pltpu.get_barrier_semaphore()
+    for peer in peers:
+        pl.semaphore_signal(barrier, inc=1, device_id={"dp": peer}, device_id_type=MESH)
+    for other in others:
+        pl.semaphore_signal(barrier, inc=1, device_id={"mp": other}, device_id_type=MESH)
+    pl.semaphore_wait(barrier, groups + ranks - 2)
+    pending = []
+
+    def remote(src, dst, send, recv, where):
+        item = pltpu.make_async_remote_copy(
+            src_ref=src, dst_ref=dst, send_sem=send, recv_sem=recv, device_id=where, device_id_type=MESH,
+        )
+        item.start()
+        pending.append(item)
+        return item
+
+    class Gather:
+        def __init__(self, ref, count, width, send, recv, own=None):
+            self.ref, self.count, self.width, self.send, self.recv, self.own = ref, count, width, send, recv, own
+            self.firsts, self.mates = {}, {}
+
+        def cut(self, chunk):
+            return pl.ds(chunk * self.width, self.width)
+
+        def copy(self, chunk, index, device, part, target, mine=False):
+            size = self.count if part is None else self.count // 2
+            shift = 0 if part is None else part * size
+            dst = self.ref.at[pl.ds(pl.multiple_of(device * self.count + shift, size), size), self.cut(chunk)]
+            src = self.own.at[pl.ds(shift, size), self.cut(chunk)] if mine and self.own is not None else dst
+            return remote(src, dst, self.send.at[chunk, index], self.recv.at[chunk, index], {"mp": target})
+
+        def begin(self, chunk):
+            x0 = self.copy(chunk, 0, me, 0, me + across, True)
+            y1 = self.copy(chunk, 4, me, 1, me + up, True)
+            x1 = self.copy(chunk, 1, me, 1, me + across, True)
+            y0 = self.copy(chunk, 3, me, 0, me + up, True)
+            self.mates[chunk] = [self.copy(chunk, 6, me, None, me + partner, True)]
+            self.firsts[chunk] = (x0, y1, x1, y0)
+
+        def forward(self, chunk):
+            x0, y1, x1, y0 = self.firsts[chunk]
+            x0.wait_recv()
+            far0 = self.copy(chunk, 5, me + across, 0, me + up)
+            y1.wait_recv()
+            far1 = self.copy(chunk, 2, me + up, 1, me + across)
+            x1.wait_recv()
+            self.mates[chunk].append(self.copy(chunk, 7, me + across, None, me + partner))
+            y0.wait_recv()
+            self.mates[chunk].append(self.copy(chunk, 8, me + up, None, me + partner))
+            self.firsts[chunk] = (far0, far1)
+
+        def corner(self, chunk):
+            far0, far1 = self.firsts[chunk]
+            far0.wait_recv()
+            self.mates[chunk].append(self.copy(chunk, 9, me + across + up, 0, me + partner))
+            far1.wait_recv()
+            self.mates[chunk].append(self.copy(chunk, 10, me + across + up, 1, me + partner))
+
+        def finish(self, chunk):
+            for item in self.mates[chunk]:
+                item.wait_recv()
+
+    mine = merged_ref.shape[0]
+    part_width = merged_ref.shape[1] // parts
+    merged_all = Gather(all_ref, mine, part_width, g_send, g_recv, merged_ref)
+    for part in range(parts):
+        merged_all.begin(part)
+    all_ref[pl.ds(pl.multiple_of(me * mine, mine), mine), :] = merged_ref[...]
+
+    slots, width = text_ref.shape
+    room = slots // groups
+    wide = width // steps
+    half = wide // 2
+
+    def iota(shape, axis):
+        return lax.broadcasted_iota(jnp.int32, shape, axis)
+
+    own = owner_ref[...]
+    eye = iota((mine, mine), 0) == iota((mine, mine), 1)
+    own_row = jnp.sum(jnp.where(eye, own.astype(jnp.float32), 0.0), axis=0, keepdims=True)
+    same = own.astype(jnp.float32) == own_row
+    before = iota((mine, mine), 0) < iota((mine, mine), 1)
+    rank_row = jnp.sum(jnp.where(same & before, 1.0, 0.0), axis=0, keepdims=True)
+    slot_row = own_row * room + rank_row
+    selected = jnp.where(iota((slots, mine), 0).astype(jnp.float32) == slot_row, 1.0, 0.0)
+    selector = selected.astype(jnp.bfloat16)
+    marks_ref[...] = jnp.broadcast_to(jnp.sum(selected, axis=1, keepdims=True), marks_ref.shape).astype(jnp.bfloat16)
+    eye = iota((slots, slots), 0) == iota((slots, slots), 1)
+    slot_col = jnp.sum(jnp.where(eye, slots_ref[...].astype(jnp.float32), 0.0), axis=1, keepdims=True)
+    picker = jnp.where(slot_col == iota((slots, slots), 1).astype(jnp.float32), 1.0, 0.0).astype(jnp.bfloat16)
+
+    def block_of(index):
+        return pl.ds(pl.multiple_of(index * room, room), room)
+
+    own_block = block_of(group)
+
+    def z_copy(index, place, src, dst):
+        return remote(src, dst, z_send.at[index, place], z_recv.at[index, place], {"dp": peers[place]})
+
+    mark_copies = [
+        z_copy(steps, place, marks_ref.at[block_of(peers[place])], arrived_marks.at[own_block])
+        for place in range(groups - 1)
+    ]
+    arrived_marks[own_block, :] = marks_ref[own_block, :]
+
+    def first(part):
+        cut = merged_all.cut(part)
+        for at, size in tiles_of(hidden_acc.shape[1]):
+            value = jnp.dot(all_ref[:, cut], w1_ref[cut, pl.ds(at, size)], preferred_element_type=jnp.float32)
+            if part:
+                value = value + hidden_acc[:, pl.ds(at, size)]
+            if part < parts - 1:
+                hidden_acc[:, pl.ds(at, size)] = value
+            else:
+                value = value + b1_ref[:, pl.ds(at, size)]
+                value = 0.5 * value * (1.0 + lax.erf(value * (2.0 ** -0.5)))
+                hidden_ref[:, pl.ds(at, size)] = value.astype(jnp.bfloat16)
+
+    for part in range(parts):
+        merged_all.forward(part)
+        if part == 0:
+            loads[0].wait()
+            loads[1].wait()
+            height = 512
+            def join(i, carry):
+                some = pl.ds(pl.multiple_of(i * height, height), height)
+                kv_ref[some, :] = jnp.concatenate([kv_raw[0, some, :], kv_raw[1, some, :]], axis=1)
+                return carry
+            lax.fori_loop(0, width // height, join, 0)
+        else:
+            merged_all.corner(part - 1)
+            merged_all.finish(part - 1)
+            first(part - 1)
+    merged_all.corner(parts - 1)
+    merged_all.finish(parts - 1)
+    first(parts - 1)
+    loads[2].wait()
+
+    devices = (me + across + up, me + across, me + up, me)
+
+    def rows_of(device):
+        return pl.ds(pl.multiple_of(device * mine, mine), mine)
+
+    reduce_mates, outward, lasts, z_copies = {}, {}, {}, {}
+
+    def r_copy(chunk, index, src, dst, target):
+        return remote(src, dst, r_send.at[chunk, index], r_recv.at[chunk, index], {"mp": target})
+
+    def halves(chunk):
+        return pl.ds(chunk * wide, half), pl.ds(chunk * wide + half, half), pl.ds(chunk * half, half)
+
+    def second(chunk):
+        for at, size in tiles_of(wide):
+            cut = pl.ds(chunk * wide + at, size)
+            partial_ref[:, cut] = jnp.dot(
+                hidden_ref[...], w2_ref[:, cut], preferred_element_type=jnp.float32
+            ).astype(jnp.bfloat16)
+        cut = pl.ds(chunk * wide, wide)
+        reduce_mates[chunk] = [
+            r_copy(chunk, slot, partial_ref.at[rows_of(devices[slot] + partner), cut], mate_ref.at[slot, :, cut], me + partner)
+            for slot in range(4)
+        ]
+
+    def add_mates(chunk):
+        low, high, small = halves(chunk)
+        cut = pl.ds(chunk * wide, wide)
+
+        def add(slot):
+            reduce_mates[chunk][slot].wait_recv()
+            partial_ref[rows_of(devices[slot]), cut] = (
+                partial_ref[rows_of(devices[slot]), cut].astype(jnp.float32) + mate_ref[slot, :, cut].astype(jnp.float32)
+            ).astype(jnp.bfloat16)
+
+        add(0)
+        far_x = r_copy(chunk, 4, partial_ref.at[rows_of(devices[0]), low], in_x.at[0, :, small], me + across)
+        far_y = r_copy(chunk, 5, partial_ref.at[rows_of(devices[0]), high], in_y.at[0, :, small], me + up)
+        add(1)
+        near_x = r_copy(chunk, 6, partial_ref.at[rows_of(devices[1]), low], in_x.at[1, :, small], me + across)
+        add(2)
+        near_y = r_copy(chunk, 7, partial_ref.at[rows_of(devices[2]), high], in_y.at[1, :, small], me + up)
+        add(3)
+        outward[chunk] = (far_x, far_y, near_x, near_y)
+
+    def via(chunk):
+        low, high, small = halves(chunk)
+        far_x, far_y, near_x, near_y = outward[chunk]
+        far_x.wait_recv()
+        partial_ref[rows_of(devices[2]), low] = (
+            partial_ref[rows_of(devices[2]), low].astype(jnp.float32) + in_x[0, :, small].astype(jnp.float32)
+        ).astype(jnp.bfloat16)
+        last_y = r_copy(chunk, 8, partial_ref.at[rows_of(devices[2]), low], last_ref.at[0, :, small], me + up)
+        far_y.wait_recv()
+        partial_ref[rows_of(devices[1]), high] = (
+            partial_ref[rows_of(devices[1]), high].astype(jnp.float32) + in_y[0, :, small].astype(jnp.float32)
+        ).astype(jnp.bfloat16)
+        last_x = r_copy(chunk, 9, partial_ref.at[rows_of(devices[1]), high], last_ref.at[1, :, small], me + across)
+        lasts[chunk] = (near_x, last_y, near_y, last_x)
+
+    def embed(chunk):
+        low, high, small = halves(chunk)
+        near_x, last_y, near_y, last_x = lasts[chunk]
+        pieces = []
+        for at, (place, near, last, side) in enumerate(((low, near_x, last_y, in_x), (high, near_y, last_x, in_y))):
+            near.wait_recv()
+            last.wait_recv()
+            total = (
+                partial_ref[rows_of(me), place].astype(jnp.float32)
+                + side[1, :, small].astype(jnp.float32) + last_ref[at, :, small].astype(jnp.float32)
+            )
+            rows = (total + b2_ref[:, place]).astype(jnp.bfloat16)
+            send_ref[:, place] = jnp.dot(selector, rows, preferred_element_type=jnp.float32).astype(jnp.bfloat16)
+        cut = pl.ds(chunk * wide, wide)
+        z_copies[chunk] = [
+            z_copy(chunk, place, send_ref.at[block_of(peers[place]), cut], arrived_ref.at[own_block, cut])
+            for place in range(groups - 1)
+        ]
+        arrived_ref[own_block, cut] = send_ref[own_block, cut]
+
+    sequence_all = Gather(rows_ref, slots, wide, a_send, a_recv)
+
+    def choose(chunk):
+        cut = pl.ds(chunk * wide, wide)
+        if chunk == 0:
+            loads[3].wait()
+            for item in mark_copies:
+                item.wait_recv()
+            own_square[...] = jnp.zeros_like(own_square)
+        image_here = jnp.dot(picker, arrived_marks[...], preferred_element_type=jnp.float32)[:, :1] > 0.5
+        for item in z_copies[chunk]:
+            item.wait_recv()
+        picked = jnp.dot(picker, arrived_ref[:, cut], preferred_element_type=jnp.float32)
+        sequence = jnp.where(image_here, picked, text_ref[:, cut].astype(jnp.float32))
+        squares = sequence * sequence
+        total = squares[:, :128]
+        for at in range(128, wide, 128):
+            total = total + squares[:, at:at + 128]
+        own_square[pl.ds(0, slots), :] += total
+        rows_ref[pl.ds(pl.multiple_of(me * slots, slots), slots), cut] = (
+            sequence * gain_ref[:, cut]
+        ).astype(jnp.bfloat16)
+        sequence_all.begin(chunk)
+
+    square_copies = []
+
+    def share_squares():
+        square_ref[me] = jnp.broadcast_to(jnp.sum(own_square[...].T, axis=0, keepdims=True), square_ref.shape[1:])
+        for place, other in enumerate(others):
+            square_copies.append(
+                remote(square_ref.at[me], square_ref.at[me], s_send.at[place], s_recv.at[place], {"mp": other})
+            )
+
+    queries = q_ref.shape[1]
+    columns = kv_ref.shape[1]
+
+    def project_into(chunk, weight_ref, at, size, shift):
+        cut = pl.ds(chunk * wide, wide)
+        value = jnp.dot(rows_ref[:, cut], weight_ref[cut, pl.ds(at, size)], preferred_element_type=jnp.float32)
+        place = pl.ds(shift + at, size)
+        if chunk:
+            value = value + acc_ref[:, place]
+        acc_ref[:, place] = value
+
+    def project_kv(chunk):
+        sequence_all.finish(chunk)
+        if chunk == 0:
+            loads[4].wait()
+        project_into(chunk, kv_ref, 0, columns, queries)
+
+    def project_q(chunk):
+        for at, size in tiles_of(queries):
+            project_into(chunk, q_ref, at, size, 0)
+
+    def stage(run, chunk):
+        if 0 <= chunk < steps:
+            run(chunk)
+
+    for step in range(steps + 6):
+        stage(second, step)
+        stage(add_mates, step - 1)
+        stage(via, step - 2)
+        stage(embed, step - 3)
+        stage(choose, step - 4)
+        if step - 4 == steps - 1:
+            share_squares()
+        stage(sequence_all.forward, step - 5)
+        stage(sequence_all.corner, step - 6)
+        stage(project_kv, step - 7)
+        stage(project_q, step - 7)
+    for item in square_copies:
+        item.wait_recv()
+    project_kv(steps - 1)
+
+    eye = iota((slots, slots), 0) == iota((slots, slots), 1)
+    scales = [
+        lax.rsqrt(
+            jnp.sum(jnp.where(eye, square_ref[rank, pl.ds(0, 1), pl.ds(0, slots)], 0.0), axis=1, keepdims=True) / width
+            + epsilon
+        )
+        for rank in range(ranks)
+    ]
+    length = ranks * slots
+    scaled = jnp.concatenate(
+        [acc_ref[pl.ds(rank * slots, slots), pl.ds(queries, columns)] * scales[rank] for rank in range(ranks)], axis=0
+    )
+    both = (scaled + kvb_ref[...]).astype(jnp.bfloat16)
+    dims = columns // (2 * KVH)
+    row = iota((columns, columns), 0)
+    wanted = (row // dims) % 2 * (dims * KVH) + row % dims * KVH + row // (2 * dims)
+    turn = jnp.where(iota((columns, columns), 1) == wanted, 1.0, 0.0).astype(jnp.bfloat16)
+    turned_ref[...] = lax.dot_general(
+        turn, both, (((1,), (1,)), ((), ())), preferred_element_type=jnp.float32
+    ).astype(jnp.bfloat16)
+    heads_here = queries // HD
+    group_size = QH // KVH
+
+    def head_rows(device):
+        return pl.ds(pl.multiple_of(device * heads_here // group_size * (2 * dims), 2 * dims), 2 * dims)
+
+    head_copies = [
+        remote(turned_ref.at[head_rows(other)], heads_ref.at[me], k_send.at[place], k_recv.at[place], {"mp": other})
+        for place, other in enumerate(others)
+    ]
+    heads_ref[me] = turned_ref[head_rows(me), :]
+    project_q(steps - 1)
+    for rank in range(ranks):
+        some = pl.ds(rank * slots, slots)
+        query_ref[some, :] = (acc_ref[some, pl.ds(0, queries)] * scales[rank] + qb_ref[...]).astype(jnp.bfloat16)
+    for item in head_copies:
+        item.wait_recv()
+    tall = 256
+    keys = heads_ref[:, pl.ds(0, dims), :].reshape(ranks * dims, length)
+    values = heads_ref[:, pl.ds(dims, dims), :].reshape(ranks * dims, length)
+    for block in range(length // tall):
+        reach = (block + 1) * tall
+        allowed = iota((tall, reach), 0) + block * tall >= iota((tall, reach), 1)
+        for head in range(heads_here):
+            place = pl.ds(head * HD, HD)
+            scores = jnp.dot(
+                query_ref[pl.ds(block * tall, tall), place], keys[:, :reach], preferred_element_type=jnp.float32
+            ) * HD ** (-0.5)
+            scores = jnp.where(allowed, scores, -1e30)
+            weights = jnp.exp(scores - jnp.max(scores, axis=-1, keepdims=True))
+            weights = (weights * (1.0 / jnp.sum(weights, axis=-1, keepdims=True))).astype(jnp.bfloat16)
+            out_ref[pl.ds(block * tall, tall), place] = lax.dot_general(
+                weights, values[:, :reach], (((1,), (1,)), ((), ())), preferred_element_type=jnp.float32
+            ).astype(jnp.bfloat16)
+    for item in pending:
+        item.wait_send()
+
+
+def fused(merged, owner, slot_of_row, text, gain, w1, b1, w2, b2, q_w, q_b, kv_w, kv_b, parts, collective_id):
+    groups, ranks = lax.axis_size("dp"), lax.axis_size("mp")
+    mine = merged.shape[0]
+    slots, width = text.shape
+    steps = STEPS
+    half = width // 2
+    queries, columns = q_w.shape[1], 2 * kv_w.shape[2]
+    length = ranks * slots
+    vmem = pl.BlockSpec(memory_space=pltpu.VMEM)
+    hbm = pl.BlockSpec(memory_space=pl.ANY)
+    dma = pltpu.SemaphoreType.DMA
+    bf16, f32 = jnp.bfloat16, jnp.float32
+    return pl.pallas_call(
+        functools.partial(fused_kernel, groups, ranks, steps, parts),
+        out_shape=jax.ShapeDtypeStruct((length, queries), bf16),
+        in_specs=[vmem] * 8 + [hbm] * 5,
+        out_specs=vmem,
+        scratch_shapes=[
+            pltpu.VMEM(w1.shape, bf16),
+            pltpu.VMEM(w2.shape, bf16),
+            pltpu.VMEM(q_w.shape, bf16),
+            pltpu.VMEM(kv_w.shape, bf16),
+            pltpu.VMEM((width, columns), bf16),
+            pltpu.VMEM((slots, width), bf16),
+            pltpu.VMEM((ranks * mine, merged.shape[1]), bf16),
+            pltpu.VMEM((ranks * mine, w1.shape[1]), f32),
+            pltpu.VMEM((ranks * mine, w1.shape[1]), bf16),
+            pltpu.VMEM((ranks * mine, width), bf16),
+            pltpu.VMEM((4, mine, width), bf16),
+            pltpu.VMEM((2, mine, half), bf16),
+            pltpu.VMEM((2, mine, half), bf16),
+            pltpu.VMEM((2, mine, half), bf16),
+            pltpu.VMEM((slots, width), bf16),
+            pltpu.VMEM((slots, width), bf16),
+            pltpu.VMEM((slots, 128), bf16),
+            pltpu.VMEM((slots, 128), bf16),
+            pltpu.VMEM((length, width), bf16),
+            pltpu.VMEM((length, queries + columns), f32),
+            pltpu.VMEM((128, 128), f32),
+            pltpu.VMEM((ranks, 8, 128), f32),
+            pltpu.VMEM((columns, length), bf16),
+            pltpu.VMEM((ranks, columns // KVH, length), bf16),
+            pltpu.VMEM((length, queries), bf16),
+            dma((5,)),
+            dma((parts, 11)), dma((parts, 11)),
+            dma((steps, 10)), dma((steps, 10)),
+            dma((steps + 1, groups - 1)), dma((steps + 1, groups - 1)),
+            dma((steps, 11)), dma((steps, 11)),
+            dma((ranks - 1,)), dma((ranks - 1,)),
+            dma((ranks - 1,)), dma((ranks - 1,)),
+        ],
+        compiler_params=pltpu.CompilerParams(collective_id=collective_id, has_side_effects=True, vmem_limit_bytes=TOP),
+        cost_estimate=pl.CostEstimate(flops=2 * length * width * (queries + columns), bytes_accessed=12 * length * width, transcendentals=0),
+    )(
+        merged, owner, slot_of_row, b1.reshape(1, -1), b2.reshape(1, -1), gain.reshape(1, -1), q_b.reshape(1, -1),
+        kv_b.reshape(1, -1), w1, w2, q_w, kv_w, text,
+    )
+
 
 def rms_norm(inputs, gain):
     inputs = inputs.astype(jnp.float32)
@@ -537,6 +977,11 @@
     merged = vision_block(
         patches, window_ids, vit_norm, vit_qkv_w, vit_qkv_b, vit_out_w, merge_norm
     )
+    if lax.axis_size("mp") == 8:
+        return fused(
+            merged, owner, slot_of_row, text_embeds, llm_norm, merge_w1, merge_b1, merge_w2, merge_b2,
+            q_w, q_b, kv_w, kv_b, merged.shape[1] // patches.shape[1], 2,
+        )
     rows_all = gather_mp(merged, 0)
     hidden = jax.nn.gelu(
         jnp.dot(rows_all, merge_w1, preferred_element_type=jnp.float32) + merge_b1,

time: 156 us -> 119 us (0.76)
  matrix products: 23.3 us -> 8.42 us
  other arithmetic: 15.3 us -> 2.07 us
  Pallas kernels: 106 us -> 97.8 us
    dot_general x3 -> x0, matrix products: 18.4 us -> none  [the longest x1 17.2 us: shards(): jnp.dot(hidden, merge_w2, preferred_element_type=jnp.float32)]
    pallas_call x4 -> x1, Pallas kernels: 106 us -> 97.8 us  [fused(): pl.pallas_call(functools.partial(fused_kernel, groups, ranks, steps, part...]
    concatenate x1 -> x0, other arithmetic: 4.09 us -> none  [shards(): kv_both = jnp.concatenate([kv_w[0], kv_w[1]], axis=1)]
    convert_element_type x5 -> x0, other arithmetic: 3.46 us -> none  [the longest x1 2.08 us: shards(): embedded = (own_rows + merge_b2).astype(jnp.bfloat16)]
    unnamed x24 -> x9, local copies, waits for them, and re-layouts: 3.85 us -> 6.4 us
    slice x2 -> x0, local copies, waits for them, and re-layouts: 2.16 us -> none  [the longest x1 1.17 us: shards(): kv_both = jnp.concatenate([kv_w[0], kv_w[1]], axis=1)]
    sub x1 -> x0, other arithmetic: 2.13 us -> none  [shards(): weights = jnp.exp(scores - peak)]
where the time goes in v1:
time: 119 us
  Pallas kernels  97.8 us (82%)
  local copies, waits for them, and re-layouts  10.2 us (9%)
  matrix products  8.42 us (7%)
  other arithmetic  2.07 us (2%)
    pallas_call x1, Pallas kernels, fused(): pl.pallas_call(functools.partial(fused_kernel, groups, ranks, steps, part...  97.8 us
    unnamed x9, local copies, waits for them, and re-layouts  6.4 us
    dot_general x1, matrix products, vision_block(): jnp.dot(normed, vit_qkv_w, preferred_element_type=jnp.float32) + vit_qkv_b  3.5 us

profile of v1, /device:TPU:0, one launch (start us, length us, event | category | flops | bytes accessed | tf_op | source)
XLA Modules:
  0.0 118.6 jit_solution(7066003181228798568)
XLA Ops:
  0.0 1.3 %reshape.124.kvb_ref = f32[1,128]{1,0:T(1,128)} reshape(f32[2,64]{1,0:T(2,128)} %param.37) | data formatting | bytes 1024 | tf_op jit(solution)/shard_map/reshape | solution.py:917
  1.3 1.1 fusion.7
  2.5 1.3 %reshape.120.b1_ref = f32[1,640]{1,0:T(1,128)} reshape(f32[640]{0:T(1024)} %param.30) | data formatting | bytes 5120 | tf_op jit(solution)/shard_map/reshape | solution.py:916
  3.7 0.8 broadcast_compare_fusion
  4.5 1.3 %copy.28.owner_ref = s32[32,1]{1,0:T(8,128)} copy(s32[32,1]{0,1:T(1,128)} %param.21) | data formatting | bytes 256 | tf_op args[2]
  5.9 0.0 copy-start
  5.9 3.5 %fusion.3 = bf16[128,1920]{1,0:T(8,128)(2,1)S(1)} fusion(bf16[1280,1920]{1,0:T(8,128)(2,1)} %param.25, f32[1920]{0:T(1024)} %param.26, bf16[128,1280]{1,0:T(8,128)(2,1)} %param.19, f32[1280]{0:T(1024)} %param.24, f32[128]{0:T(128)S(1)} %add_rsqrt_fusion.1), kind=kOutput, calls=%fused_computation.5 | convolution fusion | flops 630292480 | bytes 5747712 | tf_op jit(solution)/shard_map/dot_general | solution.py:928
  9.4 0.0 copy-start.2
  9.4 0.0 copy-start.1
  9.4 0.3 copy.26
  9.7 0.4 fusion.16
  10.1 1.1 fusion.6
  11.1 1.5 %convolution_convert_fusion = bf16[8,80,128]{2,1,0:T(8,128)(2,1)S(1)} fusion(f32[8,128]{1,0:T(8,128)S(1)} %fusion.16, bf16[1,128,3,8,80]{1,4,3,2,0:T(8,128)(2,1)S(1)} %bitcast.33, f32[8,128,128]{1,2,0:T(8,128)} %fusion.6), kind=kOutput, calls=%fused_computation.10 | convolution fusion | flops 21447808 | bytes 1380352 | tf_op jit(solution)/shard_map/bhqk,bkhd->bqhd/dot_general | solution.py:944
  12.7 0.0 copy-done
  12.7 2.0 %multiply_reduce_fusion = (f32[128]{0:T(128)S(1)}, f32[128,1280]{1,0:T(8,128)S(1)}) fusion(bf16[128,640]{0,1:T(8,128)(2,1)S(1)} %bitcast.34, bf16[640,1280]{1,0:T(8,128)(2,1)} %param.27, bf16[128,1280]{1,0:T(8,128)(2,1)S(1)} %copy-done), kind=kOutput, calls=%fused_computation.17 | convolution fusion | flops 210698112 | bytes 2785792 | tf_op jit(solution)/shard_map/dot_general | solution.py:950
  14.6 0.0 copy-done.2
  14.7 0.1 multiply_convert_fusion
  14.8 0.9 reshape.119.merged_ref
  15.7 0.0 copy-done.1
  15.7 3.2 %copy.29.kv_hbm = bf16[2,8192,64]{2,1,0:T(8,128)(2,1)} copy(bf16[2,8192,64]{1,2,0:T(8,128)(2,1)S(1)} %copy-done.1) | data formatting | bytes 4194304 | tf_op args[17]
  18.9 97.8 %shard_map.181 = bf16[512,512]{1,0:T(8,128)(2,1)} custom-call(bf16[32,5120]{1,0:T(8,128)(2,1)} %reshape.119.merged_ref, s32[32,1]{1,0:T(8,128)} %copy.28.owner_ref, s32[1,64]{1,0:T(1,128)} %slots_ref.1, f32[1,640]{1,0:T(1,128)} %reshape.120.b1_ref, f32[1,8192]{1,0:T(1,128)} %bitcast.35, f32[1,8192]{1,0:T(1,128)} %bitcast.36, f32[1,512]{1,0:T(1,128)} %bitcast.37, ...), custom_call_target="tpu_custom_call" | custom-call | flops 5368709120 | bytes 50331648 | tf_op jit(solution)/shard_map/pallas_call | solution.py:874
  116.7 1.9 %copy.32 = bf16[512,512]{1,0:T(8,128)(2,1)} copy(bf16[512,512]{1,0:T(8,128)(2,1)} %shard_map.181) | data formatting | bytes 1048576
  (2 shorter events, 0.0 us)
Async XLA Ops:
  5.9 6.8 %copy-start = (bf16[128,1280]{1,0:T(8,128)(2,1)S(1)}, bf16[128,1280]{1,0:T(8,128)(2,1)}, u32[]{:S(2)}) copy-start(bf16[128,1280]{1,0:T(8,128)(2,1)} %param.19) | copy-start | bytes 983044
  9.4 5.3 %copy-start.2 = (f32[1280]{0:T(1024)S(1)}, f32[1280]{0:T(1024)}, u32[]{:S(2)}) copy-start(f32[1280]{0:T(1024)} %param.28) | copy-start | bytes 15364
  9.4 6.3 %copy-start.1 = (bf16[2,8192,64]{1,2,0:T(8,128)(2,1)S(1)}, bf16[2,8192,64]{1,2,0:T(8,128)(2,1)}, u32[]{:S(2)}) copy-start(bf16[2,8192,64]{1,2,0:T(8,128)(2,1)} %param.36) | copy-start | bytes 6291460

commit v2 on v1

--- a/solution.py
+++ b/solution.py
@@ -477,6 +477,11 @@
 
 epsilon = 1e-06
 
+def rms_norm(inputs, gain):
+    inputs = inputs.astype(jnp.float32)
+    return inputs * lax.rsqrt(jnp.mean(inputs * inputs, axis=-1, keepdims=True) + epsilon) * gain
+
+
 STEPS = 8
 WIDE = 256
 TOP = 63 * 1024 * 1024
@@ -488,10 +493,10 @@
 
 def fused_kernel(
     groups, ranks, steps, parts,
-    merged_ref, owner_ref, slots_ref, b1_ref, b2_ref, gain_ref, qb_ref, kvb_ref,
-    w1_hbm, w2_hbm, q_hbm, kv_hbm, text_hbm,
+    ids_ref, owner_ref, slots_ref, vnorm_ref, vbias_ref, mnorm_ref, b1_ref, b2_ref, gain_ref, qb_ref, kvb_ref,
+    patches_hbm, vqkv_hbm, vout_hbm, w1_hbm, w2_hbm, q_hbm, kv_hbm, text_hbm,
     out_ref,
-    w1_ref, w2_ref, q_ref, kv_raw, kv_ref, text_ref,
+    patches_ref, vqkv_ref, vout_ref, vturn_ref, vmix_ref, w1_ref, w2_ref, q_ref, kv_ref, text_ref,
     all_ref, hidden_acc, hidden_ref, partial_ref, mate_ref, in_x, in_y, last_ref,
     send_ref, arrived_ref, marks_ref, arrived_marks, rows_ref, acc_ref, own_square, square_ref,
     turned_ref, heads_ref, query_ref,
@@ -504,18 +509,69 @@
     loads = [
         pltpu.make_async_copy(src, dst, load_sem.at[at])
         for at, (src, dst) in enumerate((
-            (w1_hbm, w1_ref), (kv_hbm, kv_raw), (w2_hbm, w2_ref), (text_hbm, text_ref), (q_hbm, q_ref),
+            (w1_hbm, w1_ref), (kv_hbm, kv_ref), (w2_hbm, w2_ref), (text_hbm, text_ref), (q_hbm, q_ref),
+            (patches_hbm, patches_ref), (vqkv_hbm, vqkv_ref), (vout_hbm, vout_ref),
         ))
     ]
-    for item in loads:
+    for item in loads[5:]:
         item.start()
     barrier = pltpu.get_barrier_semaphore()
     for peer in peers:
         pl.semaphore_signal(barrier, inc=1, device_id={"dp": peer}, device_id_type=MESH)
     for other in others:
         pl.semaphore_signal(barrier, inc=1, device_id={"mp": other}, device_id_type=MESH)
+    pending = []
+
+    def iota(shape, axis):
+        return lax.broadcasted_iota(jnp.int32, shape, axis)
+
+    def column_of(row):
+        size = row.shape[1]
+        eye = iota((size, size), 0) == iota((size, size), 1)
+        return jnp.sum(jnp.where(eye, row, 0.0), axis=1, keepdims=True)
+
+    patch_rows, vision_width = patches_ref.shape
+    mine = patch_rows // parts
+    inner = vout_ref.shape[0]
+    vision_heads = inner // VHD
+    ids_row = ids_ref[...].astype(jnp.float32)
+    in_window = column_of(ids_row) == ids_row
+    loads[5].wait()
+    normed = rms_norm(patches_ref[...], vnorm_ref[...].reshape(1, -1)).astype(jnp.bfloat16)
+    loads[6].wait()
+    for item in loads[:5]:
+        item.start()
+    for at, size in tiles_of(3 * inner):
+        value = jnp.dot(normed, vqkv_ref[:, pl.ds(at, size)], preferred_element_type=jnp.float32)
+        value = (value + vbias_ref[pl.ds(at, size)].reshape(1, -1)).astype(jnp.bfloat16).astype(jnp.float32)
+        for low in range(0, size, 128):
+            vturn_ref[pl.ds(at + low, 128), :] = value[:, low:low + 128].T.astype(jnp.bfloat16)
+    for head in range(vision_heads):
+        query, key, content = (vturn_ref[pl.ds(which * inner + head * VHD, VHD), :] for which in range(3))
+        scores = lax.dot_general(
+            key, query, (((0,), (0,)), ((), ())), preferred_element_type=jnp.float32
+        ) * VHD ** (-0.5)
+        scores = jnp.where(in_window, scores, -1e30)
+        weights = jnp.exp(scores - jnp.max(scores, axis=0, keepdims=True))
+        weights = (weights * (1.0 / jnp.sum(weights, axis=0, keepdims=True))).astype(jnp.bfloat16)
+        vmix_ref[pl.ds(head * VHD, VHD), :] = jnp.dot(content, weights, preferred_element_type=jnp.float32)
+    loads[7].wait()
+    mixed = jnp.concatenate(
+        [vmix_ref[pl.ds(at, 128), :].T.astype(jnp.bfloat16) for at in range(0, inner, 128)], axis=1
+    )
+    residual = (
+        patches_ref[...].astype(jnp.float32) + jnp.dot(mixed, vout_ref[...], preferred_element_type=jnp.float32)
+    ).astype(jnp.bfloat16)
+    merged = rms_norm(residual, mnorm_ref[...].reshape(1, -1)).astype(jnp.bfloat16)
+    row = iota((patch_rows, patch_rows), 0)
+    regroup = jnp.where(
+        iota((patch_rows, patch_rows), 1) == row % mine * parts + row // mine, 1.0, 0.0
+    ).astype(jnp.bfloat16)
+    regrouped = jnp.dot(regroup, merged, preferred_element_type=jnp.float32).astype(jnp.bfloat16)
+    own_rows = pl.ds(pl.multiple_of(me * mine, mine), mine)
+    for part in range(parts):
+        all_ref[own_rows, pl.ds(part * vision_width, vision_width)] = regrouped[part * mine:(part + 1) * mine, :]
     pl.semaphore_wait(barrier, groups + ranks - 2)
-    pending = []
 
     def remote(src, dst, send, recv, where):
         item = pltpu.make_async_remote_copy(
@@ -526,26 +582,25 @@
         return item
 
     class Gather:
-        def __init__(self, ref, count, width, send, recv, own=None):
-            self.ref, self.count, self.width, self.send, self.recv, self.own = ref, count, width, send, recv, own
+        def __init__(self, ref, count, width, send, recv):
+            self.ref, self.count, self.width, self.send, self.recv = ref, count, width, send, recv
             self.firsts, self.mates = {}, {}
 
         def cut(self, chunk):
             return pl.ds(chunk * self.width, self.width)
 
-        def copy(self, chunk, index, device, part, target, mine=False):
+        def copy(self, chunk, index, device, part, target):
             size = self.count if part is None else self.count // 2
             shift = 0 if part is None else part * size
-            dst = self.ref.at[pl.ds(pl.multiple_of(device * self.count + shift, size), size), self.cut(chunk)]
-            src = self.own.at[pl.ds(shift, size), self.cut(chunk)] if mine and self.own is not None else dst
-            return remote(src, dst, self.send.at[chunk, index], self.recv.at[chunk, index], {"mp": target})
+            ref = self.ref.at[pl.ds(pl.multiple_of(device * self.count + shift, size), size), self.cut(chunk)]
+            return remote(ref, ref, self.send.at[chunk, index], self.recv.at[chunk, index], {"mp": target})
 
         def begin(self, chunk):
-            x0 = self.copy(chunk, 0, me, 0, me + across, True)
-            y1 = self.copy(chunk, 4, me, 1, me + up, True)
-            x1 = self.copy(chunk, 1, me, 1, me + across, True)
-            y0 = self.copy(chunk, 3, me, 0, me + up, True)
-            self.mates[chunk] = [self.copy(chunk, 6, me, None, me + partner, True)]
+            x0 = self.copy(chunk, 0, me, 0, me + across)
+            y1 = self.copy(chunk, 4, me, 1, me + up)
+            x1 = self.copy(chunk, 1, me, 1, me + across)
+            y0 = self.copy(chunk, 3, me, 0, me + up)
+            self.mates[chunk] = [self.copy(chunk, 6, me, None, me + partner)]
             self.firsts[chunk] = (x0, y1, x1, y0)
 
         def forward(self, chunk):
@@ -571,33 +626,24 @@
             for item in self.mates[chunk]:
                 item.wait_recv()
 
-    mine = merged_ref.shape[0]
-    part_width = merged_ref.shape[1] // parts
-    merged_all = Gather(all_ref, mine, part_width, g_send, g_recv, merged_ref)
+    merged_all = Gather(all_ref, mine, vision_width, g_send, g_recv)
     for part in range(parts):
         merged_all.begin(part)
-    all_ref[pl.ds(pl.multiple_of(me * mine, mine), mine), :] = merged_ref[...]
 
     slots, width = text_ref.shape
     room = slots // groups
     wide = width // steps
     half = wide // 2
 
-    def iota(shape, axis):
-        return lax.broadcasted_iota(jnp.int32, shape, axis)
-
-    own = owner_ref[...]
-    eye = iota((mine, mine), 0) == iota((mine, mine), 1)
-    own_row = jnp.sum(jnp.where(eye, own.astype(jnp.float32), 0.0), axis=0, keepdims=True)
-    same = own.astype(jnp.float32) == own_row
+    own_row = owner_ref[...].astype(jnp.float32)
+    same = column_of(own_row) == own_row
     before = iota((mine, mine), 0) < iota((mine, mine), 1)
     rank_row = jnp.sum(jnp.where(same & before, 1.0, 0.0), axis=0, keepdims=True)
     slot_row = own_row * room + rank_row
     selected = jnp.where(iota((slots, mine), 0).astype(jnp.float32) == slot_row, 1.0, 0.0)
     selector = selected.astype(jnp.bfloat16)
     marks_ref[...] = jnp.broadcast_to(jnp.sum(selected, axis=1, keepdims=True), marks_ref.shape).astype(jnp.bfloat16)
-    eye = iota((slots, slots), 0) == iota((slots, slots), 1)
-    slot_col = jnp.sum(jnp.where(eye, slots_ref[...].astype(jnp.float32), 0.0), axis=1, keepdims=True)
+    slot_col = column_of(slots_ref[...].astype(jnp.float32))
     picker = jnp.where(slot_col == iota((slots, slots), 1).astype(jnp.float32), 1.0, 0.0).astype(jnp.bfloat16)
 
     def block_of(index):
@@ -623,7 +669,7 @@
             if part < parts - 1:
                 hidden_acc[:, pl.ds(at, size)] = value
             else:
-                value = value + b1_ref[:, pl.ds(at, size)]
+                value = value + b1_ref[pl.ds(at, size)].reshape(1, -1)
                 value = 0.5 * value * (1.0 + lax.erf(value * (2.0 ** -0.5)))
                 hidden_ref[:, pl.ds(at, size)] = value.astype(jnp.bfloat16)
 
@@ -631,13 +677,6 @@
         merged_all.forward(part)
         if part == 0:
             loads[0].wait()
-            loads[1].wait()
-            height = 512
-            def join(i, carry):
-                some = pl.ds(pl.multiple_of(i * height, height), height)
-                kv_ref[some, :] = jnp.concatenate([kv_raw[0, some, :], kv_raw[1, some, :]], axis=1)
-                return carry
-            lax.fori_loop(0, width // height, join, 0)
         else:
             merged_all.corner(part - 1)
             merged_all.finish(part - 1)
@@ -761,12 +800,13 @@
             )
 
     queries = q_ref.shape[1]
-    columns = kv_ref.shape[1]
-
-    def project_into(chunk, weight_ref, at, size, shift):
-        cut = pl.ds(chunk * wide, wide)
-        value = jnp.dot(rows_ref[:, cut], weight_ref[cut, pl.ds(at, size)], preferred_element_type=jnp.float32)
-        place = pl.ds(shift + at, size)
+    columns = kv_ref.shape[0]
+
+    def project_into(chunk, at, size, weight, dims):
+        value = lax.dot_general(
+            rows_ref[:, pl.ds(chunk * wide, wide)], weight, (((1,), (dims,)), ((), ())), preferred_element_type=jnp.float32
+        )
+        place = pl.ds(at, size)
         if chunk:
             value = value + acc_ref[:, place]
         acc_ref[:, place] = value
@@ -774,12 +814,13 @@
     def project_kv(chunk):
         sequence_all.finish(chunk)
         if chunk == 0:
+            loads[1].wait()
             loads[4].wait()
-        project_into(chunk, kv_ref, 0, columns, queries)
+        project_into(chunk, queries, columns, kv_ref[:, pl.ds(chunk * wide, wide)], 1)
 
     def project_q(chunk):
         for at, size in tiles_of(queries):
-            project_into(chunk, q_ref, at, size, 0)
+            project_into(chunk, at, size, q_ref[pl.ds(chunk * wide, wide), pl.ds(at, size)], 0)
 
     def stage(run, chunk):
         if 0 <= chunk < steps:
@@ -801,19 +842,15 @@
         item.wait_recv()
     project_kv(steps - 1)
 
-    eye = iota((slots, slots), 0) == iota((slots, slots), 1)
     scales = [
-        lax.rsqrt(
-            jnp.sum(jnp.where(eye, square_ref[rank, pl.ds(0, 1), pl.ds(0, slots)], 0.0), axis=1, keepdims=True) / width
-            + epsilon
-        )
-        for rank in range(ranks)
+        lax.rsqrt(column_of(square_ref[rank, pl.ds(0, 1), pl.ds(0, slots)]) / width + epsilon) for rank in range(ranks)
     ]
     length = ranks * slots
     scaled = jnp.concatenate(
         [acc_ref[pl.ds(rank * slots, slots), pl.ds(queries, columns)] * scales[rank] for rank in range(ranks)], axis=0
     )
-    both = (scaled + kvb_ref[...]).astype(jnp.bfloat16)
+    bias = jnp.concatenate([kvb_ref[pl.ds(0, 1), :], kvb_ref[pl.ds(1, 1), :]], axis=1)
+    both = (scaled + bias).astype(jnp.bfloat16)
     dims = columns // (2 * KVH)
     row = iota((columns, columns), 0)
     wanted = (row // dims) % 2 * (dims * KVH) + row % dims * KVH + row // (2 * dims)
@@ -859,9 +896,13 @@
         item.wait_send()
 
 
-def fused(merged, owner, slot_of_row, text, gain, w1, b1, w2, b2, q_w, q_b, kv_w, kv_b, parts, collective_id):
+def fused(
+    patches, window_ids, owner, slot_of_row, text, vit_norm, vit_qkv_w, vit_qkv_b, vit_out_w, merge_norm,
+    w1, b1, w2, b2, gain, q_w, q_b, kv_w, kv_b, collective_id,
+):
     groups, ranks = lax.axis_size("dp"), lax.axis_size("mp")
-    mine = merged.shape[0]
+    mine = owner.shape[0]
+    parts = patches.shape[0] // mine
     slots, width = text.shape
     steps = STEPS
     half = width // 2
@@ -874,16 +915,20 @@
     return pl.pallas_call(
         functools.partial(fused_kernel, groups, ranks, steps, parts),
         out_shape=jax.ShapeDtypeStruct((length, queries), bf16),
-        in_specs=[vmem] * 8 + [hbm] * 5,
+        in_specs=[vmem] * 11 + [hbm] * 8,
         out_specs=vmem,
         scratch_shapes=[
+            pltpu.VMEM(patches.shape, bf16),
+            pltpu.VMEM(vit_qkv_w.shape, bf16),
+            pltpu.VMEM(vit_out_w.shape, bf16),
+            pltpu.VMEM((vit_qkv_w.shape[1], patches.shape[0]), bf16),
+            pltpu.VMEM((vit_out_w.shape[0], patches.shape[0]), f32),
             pltpu.VMEM(w1.shape, bf16),
             pltpu.VMEM(w2.shape, bf16),
             pltpu.VMEM(q_w.shape, bf16),
-            pltpu.VMEM(kv_w.shape, bf16),
-            pltpu.VMEM((width, columns), bf16),
+            pltpu.VMEM((columns, width), bf16),
             pltpu.VMEM((slots, width), bf16),
-            pltpu.VMEM((ranks * mine, merged.shape[1]), bf16),
+            pltpu.VMEM((ranks * mine, w1.shape[0]), bf16),
             pltpu.VMEM((ranks * mine, w1.shape[1]), f32),
             pltpu.VMEM((ranks * mine, w1.shape[1]), bf16),
             pltpu.VMEM((ranks * mine, width), bf16),
@@ -902,7 +947,7 @@
             pltpu.VMEM((columns, length), bf16),
             pltpu.VMEM((ranks, columns // KVH, length), bf16),
             pltpu.VMEM((length, queries), bf16),
-            dma((5,)),
+            dma((8,)),
             dma((parts, 11)), dma((parts, 11)),
             dma((steps, 10)), dma((steps, 10)),
             dma((steps + 1, groups - 1)), dma((steps + 1, groups - 1)),
@@ -913,14 +958,10 @@
         compiler_params=pltpu.CompilerParams(collective_id=collective_id, has_side_effects=True, vmem_limit_bytes=TOP),
         cost_estimate=pl.CostEstimate(flops=2 * length * width * (queries + columns), bytes_accessed=12 * length * width, transcendentals=0),
     )(
-        merged, owner, slot_of_row, b1.reshape(1, -1), b2.reshape(1, -1), gain.reshape(1, -1), q_b.reshape(1, -1),
-        kv_b.reshape(1, -1), w1, w2, q_w, kv_w, text,
+        window_ids, owner.reshape(1, -1), slot_of_row, vit_norm, vit_qkv_b, merge_norm, b1,
+        b2.reshape(1, -1), gain.reshape(1, -1), q_b.reshape(1, -1), kv_b,
+        patches, vit_qkv_w, vit_out_w, w1, w2, q_w, kv_w.transpose(0, 2, 1).reshape(columns, width), text,
     )
-
-
-def rms_norm(inputs, gain):
-    inputs = inputs.astype(jnp.float32)
-    return inputs * lax.rsqrt(jnp.mean(inputs * inputs, axis=-1, keepdims=True) + epsilon) * gain
 
 
 def vision_block(patches, window_ids, vit_norm, vit_qkv_w, vit_qkv_b, vit_out_w, merge_norm):
@@ -974,14 +1015,14 @@
     kv_w,
     kv_b,
 ):
+    if lax.axis_size("mp") == 8:
+        return fused(
+            patches, window_ids, owner, slot_of_row, text_embeds, vit_norm, vit_qkv_w, vit_qkv_b, vit_out_w,
+            merge_norm, merge_w1, merge_b1, merge_w2, merge_b2, llm_norm, q_w, q_b, kv_w, kv_b, 2,
+        )
     merged = vision_block(
         patches, window_ids, vit_norm, vit_qkv_w, vit_qkv_b, vit_out_w, merge_norm
     )
-    if lax.axis_size("mp") == 8:
-        return fused(
-            merged, owner, slot_of_row, text_embeds, llm_norm, merge_w1, merge_b1, merge_w2, merge_b2,
-            q_w, q_b, kv_w, kv_b, merged.shape[1] // patches.shape[1], 2,
-        )
     rows_all = gather_mp(merged, 0)
     hidden = jax.nn.gelu(
         jnp.dot(rows_all, merge_w1, preferred_element_type=jnp.float32) + merge_b1,

time: 119 us -> 102 us (0.86)
  matrix products: 8.42 us -> 0 us
  local copies, waits for them, and re-layouts: 10.2 us -> 1.87 us
  Pallas kernels: 97.8 us -> 100 us
  other arithmetic: 2.07 us -> 0 us
    dot_general x4 -> x0, matrix products: 8.05 us -> none  [the longest x1 3.5 us: vision_block(): jnp.dot(normed, vit_qkv_w, preferred_element_type=jnp.float32) + vit_qkv_b]
    unnamed x9 -> x1, local copies, waits for them, and re-layouts: 6.4 us -> 1.87 us
    reshape x3 -> x0, local copies, waits for them, and re-layouts: 3.53 us -> none  [the longest x1 1.33 us: fused(): kv_b.reshape(1, -1)]
    pallas_call x1, Pallas kernels: 97.8 us -> 100 us  [fused(): pl.pallas_call(functools.partial(fused_kernel, groups, ranks, steps, part...]
where the time goes in v2:
time: 102 us
  Pallas kernels  100 us (98%)
  local copies, waits for them, and re-layouts  1.87 us (2%)
    pallas_call x1, Pallas kernels, fused(): pl.pallas_call(functools.partial(fused_kernel, groups, ranks, steps, part...  100 us

profile of v2, /device:TPU:0, one launch (start us, length us, event | category | flops | bytes accessed | tf_op | source)
XLA Modules:
  0.0 102.2 jit_solution(6921784256446971691)
XLA Ops:
  0.0 100.4 %shard_map.181 = bf16[512,512]{1,0:T(8,128)(2,1)} custom-call(s32[1,128]{1,0:T(1,128)} %ids_ref.1, s32[1,32]{1,0:T(1,128)} %bitcast.11, s32[1,64]{1,0:T(1,128)} %slots_ref.1, f32[1280]{0:T(1024)} %vnorm_ref.1, f32[1920]{0:T(1024)} %vbias_ref.1, f32[1280]{0:T(1024)} %mnorm_ref.1, f32[640]{0:T(1024)} %b1_ref.1, f32[1,8192]{1,0:T(1,128)} %bitcast.8, ...), custom_call_target="tpu_custom_call" | custom-call | flops 5368709120 | bytes 50331648 | tf_op jit(solution)/shard_map/pallas_call | solution.py:915
  100.4 1.9 %copy.21 = bf16[512,512]{1,0:T(8,128)(2,1)} copy(bf16[512,512]{1,0:T(8,128)(2,1)} %shard_map.181) | data formatting | bytes 1048576

commit v3 on v2

--- a/solution.py
+++ b/solution.py
@@ -493,10 +493,11 @@
 
 def fused_kernel(
     groups, ranks, steps, parts,
-    ids_ref, owner_ref, slots_ref, vnorm_ref, vbias_ref, mnorm_ref, b1_ref, b2_ref, gain_ref, qb_ref, kvb_ref,
+    ids_hbm, vnorm_hbm, vbias_hbm, mnorm_hbm, owner_hbm, slots_hbm, b1_hbm, b2_hbm, gain_hbm, qb_hbm, kvb_hbm,
     patches_hbm, vqkv_hbm, vout_hbm, w1_hbm, w2_hbm, q_hbm, kv_hbm, text_hbm,
     out_ref,
-    patches_ref, vqkv_ref, vout_ref, vturn_ref, vmix_ref, w1_ref, w2_ref, q_ref, kv_ref, text_ref,
+    ids_ref, vnorm_ref, vbias_ref, mnorm_ref, owner_ref, slots_ref, b1_ref, b2_ref, gain_ref, qb_ref, kvb_ref,
+    small_sem, patches_ref, vqkv_ref, vout_ref, vturn_ref, vmix_ref, w1_ref, w2_ref, q_ref, kv_ref, text_ref,
     all_ref, hidden_acc, hidden_ref, partial_ref, mate_ref, in_x, in_y, last_ref,
     send_ref, arrived_ref, marks_ref, arrived_marks, rows_ref, acc_ref, own_square, square_ref,
     turned_ref, heads_ref, query_ref,
@@ -513,7 +514,20 @@
             (patches_hbm, patches_ref), (vqkv_hbm, vqkv_ref), (vout_hbm, vout_ref),
         ))
     ]
-    for item in loads[5:]:
+    smalls = [
+        pltpu.make_async_copy(src, dst, small_sem.at[at])
+        for at, (src, dst) in enumerate((
+            (ids_hbm, ids_ref), (vnorm_hbm, vnorm_ref), (vbias_hbm, vbias_ref), (mnorm_hbm, mnorm_ref),
+            (owner_hbm, owner_ref), (slots_hbm, slots_ref), (b1_hbm, b1_ref), (b2_hbm, b2_ref),
+            (gain_hbm, gain_ref), (qb_hbm, qb_ref), (kvb_hbm, kvb_ref),
+        ))
+    ]
+    loads[5].start()
+    smalls[0].start()
+    smalls[1].start()
+    loads[6].start()
+    loads[7].start()
+    for item in smalls[2:]:
         item.start()
     barrier = pltpu.get_barrier_semaphore()
     for peer in peers:
@@ -534,11 +548,15 @@
     mine = patch_rows // parts
     inner = vout_ref.shape[0]
     vision_heads = inner // VHD
+    smalls[0].wait()
+    smalls[1].wait()
     ids_row = ids_ref[...].astype(jnp.float32)
     in_window = column_of(ids_row) == ids_row
     loads[5].wait()
     normed = rms_norm(patches_ref[...], vnorm_ref[...].reshape(1, -1)).astype(jnp.bfloat16)
     loads[6].wait()
+    for item in smalls[2:]:
+        item.wait()
     for item in loads[:5]:
         item.start()
     for at, size in tiles_of(3 * inner):
@@ -675,13 +693,12 @@
 
     for part in range(parts):
         merged_all.forward(part)
-        if part == 0:
-            loads[0].wait()
-        else:
-            merged_all.corner(part - 1)
+    loads[0].wait()
+    for part in range(parts):
+        merged_all.corner(part)
+        if part:
             merged_all.finish(part - 1)
             first(part - 1)
-    merged_all.corner(parts - 1)
     merged_all.finish(parts - 1)
     first(parts - 1)
     loads[2].wait()
@@ -875,23 +892,29 @@
         query_ref[some, :] = (acc_ref[some, pl.ds(0, queries)] * scales[rank] + qb_ref[...]).astype(jnp.bfloat16)
     for item in head_copies:
         item.wait_recv()
-    tall = 256
+    tall = 128
     keys = heads_ref[:, pl.ds(0, dims), :].reshape(ranks * dims, length)
     values = heads_ref[:, pl.ds(dims, dims), :].reshape(ranks * dims, length)
+    allowed = iota((tall, tall), 0) >= iota((tall, tall), 1)
     for block in range(length // tall):
         reach = (block + 1) * tall
-        allowed = iota((tall, reach), 0) + block * tall >= iota((tall, reach), 1)
+        some = pl.ds(block * tall, tall)
+        weighted = []
         for head in range(heads_here):
-            place = pl.ds(head * HD, HD)
             scores = jnp.dot(
-                query_ref[pl.ds(block * tall, tall), place], keys[:, :reach], preferred_element_type=jnp.float32
+                query_ref[some, pl.ds(head * HD, HD)], keys[:, :reach], preferred_element_type=jnp.float32
             ) * HD ** (-0.5)
-            scores = jnp.where(allowed, scores, -1e30)
+            last = jnp.where(allowed, scores[:, block * tall:], -1e30)
+            scores = jnp.concatenate([scores[:, :block * tall], last], axis=1) if block else last
             weights = jnp.exp(scores - jnp.max(scores, axis=-1, keepdims=True))
-            weights = (weights * (1.0 / jnp.sum(weights, axis=-1, keepdims=True))).astype(jnp.bfloat16)
-            out_ref[pl.ds(block * tall, tall), place] = lax.dot_general(
+            total = jnp.sum(weights, axis=-1, keepdims=True)
+            weighted.append((weights.astype(jnp.bfloat16), total))
+        out_ref[some, :] = jnp.concatenate([
+            lax.dot_general(
                 weights, values[:, :reach], (((1,), (1,)), ((), ())), preferred_element_type=jnp.float32
-            ).astype(jnp.bfloat16)
+            ) * (1.0 / total)
+            for weights, total in weighted
+        ], axis=1).astype(jnp.bfloat16)
     for item in pending:
         item.wait_send()
 
@@ -908,16 +931,20 @@
     half = width // 2
     queries, columns = q_w.shape[1], 2 * kv_w.shape[2]
     length = ranks * slots
-    vmem = pl.BlockSpec(memory_space=pltpu.VMEM)
     hbm = pl.BlockSpec(memory_space=pl.ANY)
     dma = pltpu.SemaphoreType.DMA
     bf16, f32 = jnp.bfloat16, jnp.float32
+    smalls = (
+        window_ids, vit_norm, vit_qkv_b, merge_norm, owner.reshape(1, -1), slot_of_row, b1,
+        b2.reshape(1, -1), gain.reshape(1, -1), q_b.reshape(1, -1), kv_b,
+    )
     return pl.pallas_call(
         functools.partial(fused_kernel, groups, ranks, steps, parts),
         out_shape=jax.ShapeDtypeStruct((length, queries), bf16),
-        in_specs=[vmem] * 11 + [hbm] * 8,
-        out_specs=vmem,
-        scratch_shapes=[
+        in_specs=[hbm] * 19,
+        out_specs=pl.BlockSpec(memory_space=pltpu.VMEM),
+        scratch_shapes=[pltpu.VMEM(item.shape, item.dtype) for item in smalls] + [
+            dma((len(smalls),)),
             pltpu.VMEM(patches.shape, bf16),
             pltpu.VMEM(vit_qkv_w.shape, bf16),
             pltpu.VMEM(vit_out_w.shape, bf16),
@@ -958,9 +985,7 @@
         compiler_params=pltpu.CompilerParams(collective_id=collective_id, has_side_effects=True, vmem_limit_bytes=TOP),
         cost_estimate=pl.CostEstimate(flops=2 * length * width * (queries + columns), bytes_accessed=12 * length * width, transcendentals=0),
     )(
-        window_ids, owner.reshape(1, -1), slot_of_row, vit_norm, vit_qkv_b, merge_norm, b1,
-        b2.reshape(1, -1), gain.reshape(1, -1), q_b.reshape(1, -1), kv_b,
-        patches, vit_qkv_w, vit_out_w, w1, w2, q_w, kv_w.transpose(0, 2, 1).reshape(columns, width), text,
+        *smalls, patches, vit_qkv_w, vit_out_w, w1, w2, q_w, kv_w.transpose(0, 2, 1).reshape(columns, width), text,
     )
 
 

time: 102 us -> 97.2 us (0.953)
  Pallas kernels: 100 us -> 95.1 us
    pallas_call x1, Pallas kernels: 100 us -> 95.1 us  [fused(): pl.pallas_call(functools.partial(fused_kernel, groups, ranks, steps, part...]
where the time goes in v3:
time: 97.2 us; the launch traced here: 97 us
  Pallas kernels  95.1 us (98%)
  local copies, waits for them, and re-layouts  1.87 us (2%)
    pallas_call x1, Pallas kernels, fused(): pl.pallas_call(functools.partial(fused_kernel, groups, ranks, steps, part...  95.1 us

profile of v3, /device:TPU:0, one launch (start us, length us, event | category | flops | bytes accessed | tf_op | source)
XLA Modules:
  0.0 97.0 jit_solution(7481687729929421327)
XLA Ops:
  0.0 95.1 %shard_map.181 = bf16[512,512]{1,0:T(8,128)(2,1)} custom-call(s32[1,128]{1,0:T(1,128)} %ids_hbm.1, f32[1280]{0:T(1024)} %vnorm_hbm.1, f32[1920]{0:T(1024)} %vbias_hbm.1, f32[1280]{0:T(1024)} %mnorm_hbm.1, s32[1,32]{1,0:T(1,128)} %bitcast.11, s32[1,64]{1,0:T(1,128)} %slots_hbm.1, f32[640]{0:T(1024)} %b1_hbm.1, f32[1,8192]{1,0:T(1,128)} %bitcast.8, ...), custom_call_target="tpu_custom_call" | custom-call | flops 5368709120 | bytes 50331648 | tf_op jit(solution)/shard_map/pallas_call | solution.py:941
  95.1 1.9 %copy.21 = bf16[512,512]{1,0:T(8,128)(2,1)} copy(bf16[512,512]{1,0:T(8,128)(2,1)} %shard_map.181) | data formatting | bytes 1048576

commit v4 on v3

--- a/solution.py
+++ b/solution.py
@@ -482,7 +482,7 @@
     return inputs * lax.rsqrt(jnp.mean(inputs * inputs, axis=-1, keepdims=True) + epsilon) * gain
 
 
-STEPS = 8
+UNITS = (4, 6, 6, 6, 6, 4)
 WIDE = 256
 TOP = 63 * 1024 * 1024
 
@@ -492,7 +492,7 @@
 
 
 def fused_kernel(
-    groups, ranks, steps, parts,
+    groups, ranks, spans, parts,
     ids_hbm, vnorm_hbm, vbias_hbm, mnorm_hbm, owner_hbm, slots_hbm, b1_hbm, b2_hbm, gain_hbm, qb_hbm, kvb_hbm,
     patches_hbm, vqkv_hbm, vout_hbm, w1_hbm, w2_hbm, q_hbm, kv_hbm, text_hbm,
     out_ref,
@@ -605,7 +605,7 @@
             self.firsts, self.mates = {}, {}
 
         def cut(self, chunk):
-            return pl.ds(chunk * self.width, self.width)
+            return pl.ds(*self.width[chunk])
 
         def copy(self, chunk, index, device, part, target):
             size = self.count if part is None else self.count // 2
@@ -644,14 +644,13 @@
             for item in self.mates[chunk]:
                 item.wait_recv()
 
-    merged_all = Gather(all_ref, mine, vision_width, g_send, g_recv)
+    merged_all = Gather(all_ref, mine, [(part * vision_width, vision_width) for part in range(parts)], g_send, g_recv)
     for part in range(parts):
         merged_all.begin(part)
 
     slots, width = text_ref.shape
     room = slots // groups
-    wide = width // steps
-    half = wide // 2
+    steps = len(spans)
 
     own_row = owner_ref[...].astype(jnp.float32)
     same = column_of(own_row) == own_row
@@ -714,15 +713,18 @@
         return remote(src, dst, r_send.at[chunk, index], r_recv.at[chunk, index], {"mp": target})
 
     def halves(chunk):
-        return pl.ds(chunk * wide, half), pl.ds(chunk * wide + half, half), pl.ds(chunk * half, half)
+        start, wide = spans[chunk]
+        half = wide // 2
+        return pl.ds(start, half), pl.ds(start + half, half), pl.ds(start // 2, half)
 
     def second(chunk):
+        start, wide = spans[chunk]
         for at, size in tiles_of(wide):
-            cut = pl.ds(chunk * wide + at, size)
+            cut = pl.ds(start + at, size)
             partial_ref[:, cut] = jnp.dot(
                 hidden_ref[...], w2_ref[:, cut], preferred_element_type=jnp.float32
             ).astype(jnp.bfloat16)
-        cut = pl.ds(chunk * wide, wide)
+        cut = pl.ds(*spans[chunk])
         reduce_mates[chunk] = [
             r_copy(chunk, slot, partial_ref.at[rows_of(devices[slot] + partner), cut], mate_ref.at[slot, :, cut], me + partner)
             for slot in range(4)
@@ -730,7 +732,7 @@
 
     def add_mates(chunk):
         low, high, small = halves(chunk)
-        cut = pl.ds(chunk * wide, wide)
+        cut = pl.ds(*spans[chunk])
 
         def add(slot):
             reduce_mates[chunk][slot].wait_recv()
@@ -776,17 +778,17 @@
             )
             rows = (total + b2_ref[:, place]).astype(jnp.bfloat16)
             send_ref[:, place] = jnp.dot(selector, rows, preferred_element_type=jnp.float32).astype(jnp.bfloat16)
-        cut = pl.ds(chunk * wide, wide)
+        cut = pl.ds(*spans[chunk])
         z_copies[chunk] = [
             z_copy(chunk, place, send_ref.at[block_of(peers[place]), cut], arrived_ref.at[own_block, cut])
             for place in range(groups - 1)
         ]
         arrived_ref[own_block, cut] = send_ref[own_block, cut]
 
-    sequence_all = Gather(rows_ref, slots, wide, a_send, a_recv)
+    sequence_all = Gather(rows_ref, slots, spans, a_send, a_recv)
 
     def choose(chunk):
-        cut = pl.ds(chunk * wide, wide)
+        cut = pl.ds(*spans[chunk])
         if chunk == 0:
             loads[3].wait()
             for item in mark_copies:
@@ -799,7 +801,7 @@
         sequence = jnp.where(image_here, picked, text_ref[:, cut].astype(jnp.float32))
         squares = sequence * sequence
         total = squares[:, :128]
-        for at in range(128, wide, 128):
+        for at in range(128, spans[chunk][1], 128):
             total = total + squares[:, at:at + 128]
         own_square[pl.ds(0, slots), :] += total
         rows_ref[pl.ds(pl.multiple_of(me * slots, slots), slots), cut] = (
@@ -821,7 +823,7 @@
 
     def project_into(chunk, at, size, weight, dims):
         value = lax.dot_general(
-            rows_ref[:, pl.ds(chunk * wide, wide)], weight, (((1,), (dims,)), ((), ())), preferred_element_type=jnp.float32
+            rows_ref[:, pl.ds(*spans[chunk])], weight, (((1,), (dims,)), ((), ())), preferred_element_type=jnp.float32
         )
         place = pl.ds(at, size)
         if chunk:
@@ -833,28 +835,28 @@
         if chunk == 0:
             loads[1].wait()
             loads[4].wait()
-        project_into(chunk, queries, columns, kv_ref[:, pl.ds(chunk * wide, wide)], 1)
+        project_into(chunk, queries, columns, kv_ref[:, pl.ds(*spans[chunk])], 1)
 
     def project_q(chunk):
         for at, size in tiles_of(queries):
-            project_into(chunk, at, size, q_ref[pl.ds(chunk * wide, wide), pl.ds(at, size)], 0)
+            project_into(chunk, at, size, q_ref[pl.ds(*spans[chunk]), pl.ds(at, size)], 0)
 
     def stage(run, chunk):
         if 0 <= chunk < steps:
             run(chunk)
 
-    for step in range(steps + 6):
-        stage(second, step)
+    for step in range(steps + 7):
+        stage(second, step - 0)
         stage(add_mates, step - 1)
         stage(via, step - 2)
         stage(embed, step - 3)
-        stage(choose, step - 4)
-        if step - 4 == steps - 1:
+        stage(choose, step - 5)
+        if step - 5 == steps - 1:
             share_squares()
-        stage(sequence_all.forward, step - 5)
-        stage(sequence_all.corner, step - 6)
-        stage(project_kv, step - 7)
-        stage(project_q, step - 7)
+        stage(sequence_all.forward, step - 6)
+        stage(sequence_all.corner, step - 7)
+        stage(project_kv, step - 8)
+        stage(project_q, step - 8)
     for item in square_copies:
         item.wait_recv()
     project_kv(steps - 1)
@@ -927,7 +929,9 @@
     mine = owner.shape[0]
     parts = patches.shape[0] // mine
     slots, width = text.shape
-    steps = STEPS
+    unit = width // sum(UNITS)
+    spans = [(sum(UNITS[:at]) * unit, size * unit) for at, size in enumerate(UNITS)]
+    steps = len(spans)
     half = width // 2
     queries, columns = q_w.shape[1], 2 * kv_w.shape[2]
     length = ranks * slots
@@ -939,7 +943,7 @@
         b2.reshape(1, -1), gain.reshape(1, -1), q_b.reshape(1, -1), kv_b,
     )
     return pl.pallas_call(
-        functools.partial(fused_kernel, groups, ranks, steps, parts),
+        functools.partial(fused_kernel, groups, ranks, spans, parts),
         out_shape=jax.ShapeDtypeStruct((length, queries), bf16),
         in_specs=[hbm] * 19,
         out_specs=pl.BlockSpec(memory_space=pltpu.VMEM),

time: 97.2 us -> 93.6 us (0.963)
  Pallas kernels: 95.1 us -> 91.5 us
    pallas_call x1, Pallas kernels: 95.1 us -> 91.5 us  [fused(): pl.pallas_call(functools.partial(fused_kernel, groups, ranks, spans, part...]
where the time goes in v4:
time: 93.6 us; the launch traced here: 93.4 us
  Pallas kernels  91.5 us (98%)
  local copies, waits for them, and re-layouts  1.87 us (2%)
    pallas_call x1, Pallas kernels, fused(): pl.pallas_call(functools.partial(fused_kernel, groups, ranks, spans, part...  91.5 us

profile of v4, /device:TPU:0, one launch (start us, length us, event | category | flops | bytes accessed | tf_op | source)
XLA Modules:
  0.0 93.4 jit_solution(8488104570857581224)
XLA Ops:
  0.0 91.5 %shard_map.181 = bf16[512,512]{1,0:T(8,128)(2,1)} custom-call(s32[1,128]{1,0:T(1,128)} %ids_hbm.1, f32[1280]{0:T(1024)} %vnorm_hbm.1, f32[1920]{0:T(1024)} %vbias_hbm.1, f32[1280]{0:T(1024)} %mnorm_hbm.1, s32[1,32]{1,0:T(1,128)} %bitcast.11, s32[1,64]{1,0:T(1,128)} %slots_hbm.1, f32[640]{0:T(1024)} %b1_hbm.1, f32[1,8192]{1,0:T(1,128)} %bitcast.8, ...), custom_call_target="tpu_custom_call" | custom-call | flops 5368709120 | bytes 50331648 | tf_op jit(solution)/shard_map/pallas_call | solution.py:945
  91.5 1.9 %copy.21 = bf16[512,512]{1,0:T(8,128)(2,1)} copy(bf16[512,512]{1,0:T(8,128)(2,1)} %shard_map.181) | data formatting | bytes 1048576

commit v5 on v4

--- a/solution.py
+++ b/solution.py
@@ -564,15 +564,21 @@
         value = (value + vbias_ref[pl.ds(at, size)].reshape(1, -1)).astype(jnp.bfloat16).astype(jnp.float32)
         for low in range(0, size, 128):
             vturn_ref[pl.ds(at + low, 128), :] = value[:, low:low + 128].T.astype(jnp.bfloat16)
-    for head in range(vision_heads):
-        query, key, content = (vturn_ref[pl.ds(which * inner + head * VHD, VHD), :] for which in range(3))
-        scores = lax.dot_general(
-            key, query, (((0,), (0,)), ((), ())), preferred_element_type=jnp.float32
-        ) * VHD ** (-0.5)
-        scores = jnp.where(in_window, scores, -1e30)
+    def third(which, head):
+        return vturn_ref[pl.ds(which * inner + head * VHD, VHD), :]
+
+    all_scores = [
+        jnp.where(in_window, lax.dot_general(
+            third(1, head), third(0, head), (((0,), (0,)), ((), ())), preferred_element_type=jnp.float32
+        ) * VHD ** (-0.5), -1e30)
+        for head in range(vision_heads)
+    ]
+    all_weights = []
+    for scores in all_scores:
         weights = jnp.exp(scores - jnp.max(scores, axis=0, keepdims=True))
-        weights = (weights * (1.0 / jnp.sum(weights, axis=0, keepdims=True))).astype(jnp.bfloat16)
-        vmix_ref[pl.ds(head * VHD, VHD), :] = jnp.dot(content, weights, preferred_element_type=jnp.float32)
+        all_weights.append((weights * (1.0 / jnp.sum(weights, axis=0, keepdims=True))).astype(jnp.bfloat16))
+    for head, weights in enumerate(all_weights):
+        vmix_ref[pl.ds(head * VHD, VHD), :] = jnp.dot(third(2, head), weights, preferred_element_type=jnp.float32)
     loads[7].wait()
     mixed = jnp.concatenate(
         [vmix_ref[pl.ds(at, 128), :].T.astype(jnp.bfloat16) for at in range(0, inner, 128)], axis=1
@@ -644,7 +650,8 @@
             for item in self.mates[chunk]:
                 item.wait_recv()
 
-    merged_all = Gather(all_ref, mine, [(part * vision_width, vision_width) for part in range(parts)], g_send, g_recv)
+    merged_all = Gather(all_ref, mine, [(part * 2 * vision_width, 2 * vision_width) for part in range(parts // 2)], g_send, g_recv)
+    parts = parts // 2
     for part in range(parts):
         merged_all.begin(part)
 
@@ -850,25 +857,25 @@
         stage(add_mates, step - 1)
         stage(via, step - 2)
         stage(embed, step - 3)
+        stage(project_kv, step - 8)
+        stage(project_q, step - 8)
         stage(choose, step - 5)
         if step - 5 == steps - 1:
             share_squares()
         stage(sequence_all.forward, step - 6)
         stage(sequence_all.corner, step - 7)
-        stage(project_kv, step - 8)
-        stage(project_q, step - 8)
     for item in square_copies:
         item.wait_recv()
-    project_kv(steps - 1)
 
     scales = [
         lax.rsqrt(column_of(square_ref[rank, pl.ds(0, 1), pl.ds(0, slots)]) / width + epsilon) for rank in range(ranks)
     ]
+    bias = jnp.concatenate([kvb_ref[pl.ds(0, 1), :], kvb_ref[pl.ds(1, 1), :]], axis=1)
     length = ranks * slots
+    project_kv(steps - 1)
     scaled = jnp.concatenate(
         [acc_ref[pl.ds(rank * slots, slots), pl.ds(queries, columns)] * scales[rank] for rank in range(ranks)], axis=0
     )
-    bias = jnp.concatenate([kvb_ref[pl.ds(0, 1), :], kvb_ref[pl.ds(1, 1), :]], axis=1)
     both = (scaled + bias).astype(jnp.bfloat16)
     dims = columns // (2 * KVH)
     row = iota((columns, columns), 0)
@@ -901,16 +908,16 @@
     for block in range(length // tall):
         reach = (block + 1) * tall
         some = pl.ds(block * tall, tall)
+        block_scores = [
+            jnp.dot(query_ref[some, pl.ds(head * HD, HD)], keys[:, :reach], preferred_element_type=jnp.float32)
+            for head in range(heads_here)
+        ]
         weighted = []
-        for head in range(heads_here):
-            scores = jnp.dot(
-                query_ref[some, pl.ds(head * HD, HD)], keys[:, :reach], preferred_element_type=jnp.float32
-            ) * HD ** (-0.5)
+        for scores in block_scores:
             last = jnp.where(allowed, scores[:, block * tall:], -1e30)
             scores = jnp.concatenate([scores[:, :block * tall], last], axis=1) if block else last
-            weights = jnp.exp(scores - jnp.max(scores, axis=-1, keepdims=True))
-            total = jnp.sum(weights, axis=-1, keepdims=True)
-            weighted.append((weights.astype(jnp.bfloat16), total))
+            weights = jnp.exp((scores - jnp.max(scores, axis=-1, keepdims=True)) * HD ** (-0.5))
+            weighted.append((weights.astype(jnp.bfloat16), jnp.sum(weights, axis=-1, keepdims=True)))
         out_ref[some, :] = jnp.concatenate([
             lax.dot_general(
                 weights, values[:, :reach], (((1,), (1,)), ((), ())), preferred_element_type=jnp.float32

time: 93.6 us -> 93 us (level)
  no operation moved by 1% of the time
where the time goes in v5:
time: 93 us; the launch traced here: 92.8 us
  Pallas kernels  90.9 us (98%)
  local copies, waits for them, and re-layouts  1.87 us (2%)
    pallas_call x1, Pallas kernels, fused(): pl.pallas_call(functools.partial(fused_kernel, groups, ranks, spans, part...  90.9 us
    unnamed x1, local copies, waits for them, and re-layouts  1.87 us

profile of v5, /device:TPU:0, one launch (start us, length us, event | category | flops | bytes accessed | tf_op | source)
XLA Modules:
  0.0 92.8 jit_solution(3476389584105299682)
XLA Ops:
  0.0 90.9 %shard_map.181 = bf16[512,512]{1,0:T(8,128)(2,1)} custom-call(s32[1,128]{1,0:T(1,128)} %ids_hbm.1, f32[1280]{0:T(1024)} %vnorm_hbm.1, f32[1920]{0:T(1024)} %vbias_hbm.1, f32[1280]{0:T(1024)} %mnorm_hbm.1, s32[1,32]{1,0:T(1,128)} %bitcast.11, s32[1,64]{1,0:T(1,128)} %slots_hbm.1, f32[640]{0:T(1024)} %b1_hbm.1, f32[1,8192]{1,0:T(1,128)} %bitcast.8, ...), custom_call_target="tpu_custom_call" | custom-call | flops 5368709120 | bytes 50331648 | tf_op jit(solution)/shard_map/pallas_call | solution.py:952
  91.0 1.9 %copy.21 = bf16[512,512]{1,0:T(8,128)(2,1)} copy(bf16[512,512]{1,0:T(8,128)(2,1)} %shard_map.181) | data formatting | bytes 1048576
